TPU v7x, 32 devices: a whole 2x2x4 slice. The times are simulated.
32 devices in a mesh: shell: 2 (over x), pix: 16 (over z, y, core).
Axes of the slice: x: 2, y: 2, z: 4, core: 2. Of those that a mesh axis runs over, the one named last changes fastest.
Arguments:
- block_tile: int32 [4, 1024], P('shell'), may hold values from 0 to 2047, as said below
- cell_index: int32 [4, 1024, 512], P('shell', 'pix'), may hold values from 0 to 2047
- masses: bfloat16 [4, 1024, 512], P('shell', 'pix'), may hold values from 0.125 to 8, as said below
- plane_coef: float32 [4], P('shell'), may hold values from 0.1 to 0.4
- plane_dist: float32 [4], P('shell'), may hold values from 0.2 to 1
- source_inv: float32 [4], P('shell'), may hold values from 0.5 to 1
Outputs:
- convergence: float32 [4, 2048, 2048], P('shell', 'pix')
- shear_one: float32 [4, 2048, 2048], P('shell', 'pix')
- shear_two: float32 [4, 2048, 2048], P('shell', 'pix')
Inputs may be any that keep to these rules, and one draw needn't show every extreme that they name: `block_tile`: each row is 16 aligned runs of 64 entries, one run per index of pix. The entries of a run are distinct, and at most 8 of them lie in one index's rows of tiles (tile b lies in the rows of index b // 128). In every plane some index receives exactly 8 tiles from every run. `masses`: positive particle weights.
All inputs are finite; a program needn't handle non-finite values.
Results may differ from a plain program's by a relative error of at most 0.0003.
Values sent between devices are 32-bit elements; how exact they have to be, the bound alone decides.
A program may use at most 64 MiB of HBM per device.

v0:
```python
from functools import partial
import math

import jax
import jax.numpy as jnp
from jax import lax
from jax.sharding import PartitionSpec as P

L = 2048
TR = 16
TC = 128


HIGHEST = lax.Precision.HIGHEST


def entering(value, axis, join, neutral):
    count, mine = (lax.axis_size(axis), lax.axis_index(axis))
    pieces = jax.tree.map(lambda part: lax.all_gather(part, axis), value)
    running = jax.tree.map(
        lambda part, zero: jnp.full_like(part, 0) + jnp.asarray(zero, part.dtype), value, neutral
    )

    def lap(position, running):
        longer = join(running, jax.tree.map(lambda part: part[position], pieces))
        return jax.tree.map(lambda new, old: jnp.where(position < mine, new, old), longer, running)

    return lax.fori_loop(0, count - 1, lap, running)


def dft_table(left_size, right_size, period, sign_value):
    left_idx = jnp.arange(left_size)[:, None]
    right_idx = jnp.arange(right_size)[None, :]
    angle = 2.0 * math.pi / period * (left_idx * right_idx % period).astype(jnp.float32)
    return (jnp.cos(angle), sign_value * jnp.sin(angle))


def mix_outer(table, real_part, imag_part):
    cosine, sine_part = table
    contract = partial(jnp.einsum, "ab,...bc->...ac", precision=HIGHEST)
    return (
        contract(cosine, real_part) - contract(sine_part, imag_part),
        contract(sine_part, real_part) + contract(cosine, imag_part),
    )


def mix_inner(table, real_part, imag_part):
    cosine, sine_part = table
    product = partial(jnp.matmul, precision=HIGHEST)
    return (
        product(real_part, cosine) - product(imag_part, sine_part),
        product(real_part, sine_part) + product(imag_part, cosine),
    )


def twist(table, real_part, imag_part):
    cosine, sine_part = table
    return (real_part * cosine - imag_part * sine_part, real_part * sine_part + imag_part * cosine)


def transform_last(real_part, imag_part, sign_value):
    length = real_part.shape[-1]
    inner = math.gcd(length, 128)
    outer = length // inner
    leading = real_part.shape[:-1]
    real_part = real_part.reshape(leading + (outer, inner))
    imag_part = imag_part.reshape(leading + (outer, inner))
    outer_table = dft_table(outer, outer, outer, sign_value)
    inner_table = dft_table(inner, inner, inner, sign_value)
    twiddle = dft_table(outer, inner, length, sign_value)
    if sign_value < 0:
        real_part, imag_part = mix_outer(outer_table, real_part, imag_part)
        real_part, imag_part = twist(twiddle, real_part, imag_part)
        real_part, imag_part = mix_inner(inner_table, real_part, imag_part)
    else:
        real_part, imag_part = mix_inner(inner_table, real_part, imag_part)
        real_part, imag_part = twist(twiddle, real_part, imag_part)
        real_part, imag_part = mix_outer(outer_table, real_part, imag_part)
    return (real_part.reshape(leading + (length,)), imag_part.reshape(leading + (length,)))


def frequency_of(position, length):
    inner = math.gcd(length, 128)
    outer = length // inner
    frequency = position // inner + outer * (position % inner)
    signed = jnp.where(frequency >= length // 2, frequency - length, frequency).astype(jnp.float32)
    keep_mask = (frequency != length // 2).astype(jnp.float32)
    return (signed, keep_mask)


def add_pairs(earlier_pair, later_pair):
    return (earlier_pair[0] + later_pair[0], earlier_pair[1] + later_pair[1])


def deposit_group(item):
    cell_ids, weights = item
    tile_rows = cell_ids // TC
    tile_cols = cell_ids % TC
    row_hot = jnp.where(
        tile_rows[:, None, :] == jnp.arange(TR)[None, :, None],
        weights[:, None, :],
        jnp.zeros((), jnp.bfloat16),
    )
    col_hot = (tile_cols[:, :, None] == jnp.arange(TC)[None, None, :]).astype(jnp.bfloat16)
    return jnp.einsum("grk,gkc->grc", row_hot, col_hot, preferred_element_type=jnp.float32)


def rows_to_sending(packed, groups, slab, cols_own):
    count, fields = (packed.shape[0], packed.shape[1])
    return (
        packed.reshape(count, fields, slab, groups, cols_own)
        .transpose(3, 0, 1, 4, 2)
        .reshape(groups, count, fields, cols_own * slab)
    )


def arrived_to_columns(arrived, groups, slab, cols_own):
    count, fields = (arrived.shape[1], arrived.shape[2])
    return (
        arrived.reshape(groups, count, fields, cols_own, slab)
        .transpose(1, 2, 3, 0, 4)
        .reshape(count, fields, cols_own, groups * slab)
    )


def columns_to_sending(stacked, groups, slab, cols_own):
    count, fields = (stacked.shape[0], stacked.shape[1])
    return (
        stacked.reshape(count, fields, cols_own, groups, slab)
        .transpose(3, 0, 1, 2, 4)
        .reshape(groups, count, fields, cols_own * slab)
    )


def landed_to_rows(landed, groups, slab, cols_own):
    count, fields = (landed.shape[1], landed.shape[2])
    return (
        landed.reshape(groups, count, fields, cols_own, slab)
        .transpose(1, 2, 4, 0, 3)
        .reshape(count, fields, slab, groups * cols_own)
    )


def local(block_tile, cell_index, masses, plane_coef, plane_dist, source_inv):
    groups = lax.axis_size("pix")
    my_index = lax.axis_index("pix")
    planes, local_tiles, per_tile = cell_index.shape
    slab = L // groups
    per_owner = slab // TR * (L // TC)
    cap = max(1, 2 * local_tiles // groups)
    flat = TR * TC
    batch_tiles = 8
    deposited = lax.map(
        deposit_group,
        (cell_index.reshape(-1, batch_tiles, per_tile), masses.reshape(-1, batch_tiles, per_tile)),
    )
    tile_sums = deposited.reshape(planes, local_tiles, flat)
    table = block_tile.reshape(planes, groups, local_tiles)
    owner = table // per_owner
    earlier = jnp.arange(local_tiles)[:, None] < jnp.arange(local_tiles)[None, :]
    same_owner = owner[:, :, :, None] == owner[:, :, None, :]
    rank = jnp.sum(jnp.where(same_owner & earlier[None, None], 1, 0), axis=2)
    slot = owner * cap + rank
    my_slots = lax.dynamic_index_in_dim(slot, my_index, axis=1, keepdims=False)
    slot_grid = jnp.arange(groups)[:, None] * cap + jnp.arange(cap)[None, :]
    send_hot = (my_slots[:, None, None, :] == slot_grid[None, :, :, None]).astype(jnp.float32)
    outgoing = jnp.einsum("pnct,ptf->npcf", send_hot, tile_sums, precision=HIGHEST)
    incoming = lax.all_to_all(outgoing, "pix", split_axis=0, concat_axis=0, tiled=True)
    local_index = table - my_index * per_owner
    is_mine = owner == my_index
    tile_hot = (is_mine[..., None] & (local_index[..., None] == jnp.arange(per_owner))).astype(
        jnp.float32
    )
    slot_hot = (rank[..., None] == jnp.arange(cap)).astype(jnp.float32)
    placing = jnp.einsum("pstl,pstc->plsc", tile_hot, slot_hot, precision=HIGHEST)
    slab_tiles = jnp.einsum("plsc,spcf->plf", placing, incoming, precision=HIGHEST)
    density = (
        slab_tiles.reshape(planes, slab // TR, L // TC, TR, TC)
        .transpose(0, 1, 3, 2, 4)
        .reshape(planes, slab, L)
    )
    total = lax.psum(jnp.sum(density, axis=(1, 2)), "pix")
    contrast = density / (total / (L * L))[:, None, None] - 1.0
    near_local = jnp.cumsum(plane_coef[:, None, None] * contrast, axis=0)
    far_local = jnp.cumsum((plane_coef * plane_dist)[:, None, None] * contrast, axis=0)
    blank = jnp.zeros((slab, L), jnp.float32)
    near_before, far_before = entering(
        (near_local[-1], far_local[-1]), "shell", add_pairs, (blank, blank)
    )
    convergence = near_before + near_local - source_inv[:, None, None] * (far_before + far_local)
    cols_own = L // groups
    wave_x, keep_x = frequency_of(my_index * cols_own + jnp.arange(cols_own), L)
    wave_y, keep_y = frequency_of(jnp.arange(L), L)
    wave_x = wave_x[:, None]
    wave_y = wave_y[None, :]
    both_keep = keep_x[:, None] * keep_y[None, :]
    wave_power = jnp.maximum(wave_x * wave_x + wave_y * wave_y, 1.0)
    kernel_one = both_keep * (wave_x * wave_x - wave_y * wave_y) / wave_power
    kernel_two = both_keep * 2.0 * wave_x * wave_y / wave_power
    scale = 1.0 / (L * L)
    spec_real, spec_imag = transform_last(convergence[0::2], convergence[1::2], -1.0)
    sending = rows_to_sending(jnp.stack([spec_real, spec_imag], axis=1), groups, slab, cols_own)
    arrived = lax.all_to_all(sending, "pix", split_axis=0, concat_axis=0, tiled=True)
    columns = arrived_to_columns(arrived, groups, slab, cols_own)
    row_real, row_imag = transform_last(columns[:, 0], columns[:, 1], -1.0)
    first_real, first_imag = transform_last(row_real * kernel_one, row_imag * kernel_one, 1.0)
    second_real, second_imag = transform_last(row_real * kernel_two, row_imag * kernel_two, 1.0)
    stacked = jnp.stack([first_real, first_imag, second_real, second_imag], axis=1)
    landed = lax.all_to_all(
        columns_to_sending(stacked, groups, slab, cols_own),
        "pix",
        split_axis=0,
        concat_axis=0,
        tiled=True,
    )
    row_layout = landed_to_rows(landed, groups, slab, cols_own)
    even_one, odd_one = transform_last(row_layout[:, 0], row_layout[:, 1], 1.0)
    even_two, odd_two = transform_last(row_layout[:, 2], row_layout[:, 3], 1.0)
    shear_one = jnp.stack([even_one, odd_one], axis=1).reshape(planes, slab, L)
    shear_two = jnp.stack([even_two, odd_two], axis=1).reshape(planes, slab, L)
    return (convergence, shear_one * scale, shear_two * scale)


def solution(mesh):
    placed = (
        P("shell", None),
        P("shell", "pix", None),
        P("shell", "pix", None),
        P("shell"),
        P("shell"),
        P("shell"),
    )
    return jax.shard_map(
        local,
        mesh=mesh,
        in_specs=placed,
        out_specs=(P("shell", "pix", None), P("shell", "pix", None), P("shell", "pix", None)),
        check_vma=False,
    )
```

profile of v0, /device:TPU:1, one launch (start us, length us, event | category | flops | bytes accessed | tf_op | source)
XLA Modules:
  0.0 498.4 jit_solution(13083244063688740668)
XLA Ops:
  8.0 56.0 %while.8 = (s32[]{:T(128)}, f32[16,8,16,128]{3,2,1,0:T(8,128)S(1)}, s32[16,8,512]{2,1,0:T(8,128)}, bf16[16,8,512]{2,1,0:T(8,128)(2,1)}, s32[]{:T(128)}) while((s32[]{:T(128)}, f32[16,8,16,128]{3,2,1,0:T(8,128)S(1)}, s32[16,8,512]{2,1,0:T(8,128)}, bf16[16,8,512]{2,1,0:T(8,128)(2,1)}, s32[]{:T(128)}) %tuple.63), condition=%wide.region_2.3_spmd, body=%wide.region_1.2_spmd.sunk | while | flops 17534976 | bytes 196693 | solution.py:153
  65.7 2.5 copy.183
  68.2 7.3 %all-to-all-start = ((f32[16,2,8,2048]{3,2,1,0:T(8,128)}), f32[16,2,8,2048]{3,2,1,0:T(8,128)S(1)}, u32[]{:S(2)}, u32[]{:S(2)}) async-start(f32[16,2,8,2048]{3,2,1,0:T(8,128)} %copy.183), calls=%async_computation | async-start | bytes 4194304 | tf_op jit(solution)/shard_map/all_to_all | solution.py:168
  76.9 40.2 %all-to-all-done = f32[16,2,8,2048]{3,2,1,0:T(8,128)S(1)} async-done(((f32[16,2,8,2048]{3,2,1,0:T(8,128)}), f32[16,2,8,2048]{3,2,1,0:T(8,128)S(1)}, u32[]{:S(2)}, u32[]{:S(2)}) %all-to-all-start) | async-done | bytes 2097184 | tf_op jit(solution)/shard_map/all_to_all | solution.py:168
  117.1 3.2 bitcast_reduce_fusion
  120.3 33.9 %psum.7 = f32[2]{0:T(128)S(1)} all-reduce(f32[2]{0:T(128)S(1)} %get-tuple-element.117), channel_id=1, replica_groups=mesh['shell'=2,'pix'=16] {'pix'}, use_global_device_ids=true, to_apply=%region_4.5 | all-reduce | flops 2 | bytes 16 | tf_op jit(solution)/shard_map/psum | solution.py:182
  154.2 2.0 copy.236
  156.2 2.0 copy.185
  165.7 31.5 %all-gather.3.cloned.1.call-done = f32[2,128,2048]{2,1,0:T(8,128)} async-done(((f32[1,128,2048]{2,1,0:T(8,128)}), f32[2,128,2048]{2,1,0:T(8,128)}) %all-gather.3.cloned.1.call-update) | async-done | bytes 2097168 | tf_op jit(solution)/shard_map/all_gather | solution.py:19
  198.6 33.9 %all-gather.5.cloned.1.call-done = f32[2,128,2048]{2,1,0:T(8,128)} async-done(((f32[1,128,2048]{2,1,0:T(8,128)}), f32[2,128,2048]{2,1,0:T(8,128)}) %all-gather.5.cloned.1.call-update) | async-done | bytes 2097168 | tf_op jit(solution)/shard_map/all_gather | solution.py:19
  245.7 2.0 fusion.31
  249.7 6.4 %all-to-all-start.1 = ((f32[16,1,2,16384]{3,1,2,0:T(1,128)}), f32[16,1,2,16384]{3,1,2,0:T(1,128)S(1)}, u32[]{:S(2)}, u32[]{:S(2)}) async-start(f32[16,1,2,16384]{3,1,2,0:T(1,128)} %bitcast.319), calls=%async_computation.1 | async-start | bytes 4194304 | tf_op jit(solution)/shard_map/all_to_all | solution.py:203
  256.2 41.4 %all-to-all-done.1 = f32[16,1,2,16384]{3,1,2,0:T(1,128)S(1)} async-done(((f32[16,1,2,16384]{3,1,2,0:T(1,128)}), f32[16,1,2,16384]{3,1,2,0:T(1,128)S(1)}, u32[]{:S(2)}, u32[]{:S(2)}) %all-to-all-start.1) | async-done | bytes 2097184 | tf_op jit(solution)/shard_map/all_to_all | solution.py:203
  299.4 2.6 fusion.465
  324.5 1.9 multiply_add_fusion.3
  326.4 2.0 fusion.65
  341.7 103.1 %all_to_all.15 = f32[16,1,4,16384]{3,1,2,0:T(1,128)S(1)} all-to-all(f32[16,1,4,16384]{3,1,2,0:T(1,128)S(1)} %bitcast.304), channel_id=1, replica_groups=mesh['shell'=2,'pix'=16] {'pix'}, dimensions={0} | all-to-all | bytes 8388608 | tf_op jit(solution)/shard_map/all_to_all | solution.py:209
  445.6 1.9 fusion.91
  447.6 1.9 fusion.108
  449.5 1.9 fusion.94
  451.4 1.9 fusion.111
  453.4 2.0 convolution_subtract_fusion.3
  455.4 2.2 convolution_add_fusion.3
  457.5 2.0 convolution_subtract_fusion.1
  459.5 2.3 multiply_add_fusion
  468.3 2.8 fusion.22
  471.2 2.6 fusion.21
  473.8 2.4 stack_reshape.21
  476.2 2.4 stack_reshape.20
  478.5 2.6 fusion.24
  481.1 2.6 fusion.23
  483.7 2.5 stack_reshape.9
  (170 shorter events, 133.2 us)
Async XLA Ops:
  68.2 48.9 %all-to-all-start = ((f32[16,2,8,2048]{3,2,1,0:T(8,128)}), f32[16,2,8,2048]{3,2,1,0:T(8,128)S(1)}, u32[]{:S(2)}, u32[]{:S(2)}) async-start(f32[16,2,8,2048]{3,2,1,0:T(8,128)} %copy.183), calls=%async_computation | async-start | bytes 4194304 | tf_op jit(solution)/shard_map/all_to_all | solution.py:168
  75.6 121.7 %all-gather.3.cloned.1.call-start = ((), (), s32[]{:S(2)}) async-start(), calls=%async_computation.3 | async-start | bytes 3145728 | tf_op jit(solution)/shard_map/all_gather | solution.py:19
  158.2 1.7 copy-start.10
  160.2 1.3 copy-start
  161.6 1.4 copy-start.12
  162.7 69.9 %all-gather.5.cloned.1.call-start = ((), (), s32[]{:S(2)}) async-start(), calls=%async_computation.4 | async-start | bytes 3145728 | tf_op jit(solution)/shard_map/all_gather | solution.py:19
  163.3 1.3 copy-start.2
  165.7 68.3 %copy-start.1 = (f32[2,128,2048]{2,1,0:T(8,128)S(1)}, f32[2,128,2048]{2,1,0:T(8,128)}, u32[]{:S(2)}) copy-start(f32[2,128,2048]{2,1,0:T(8,128)} %copy-done) | copy-start | bytes 6291460
  165.7 68.3 %copy-start.11 = (f32[2]{0:T(128)S(1)}, f32[2]{0:T(128)}, u32[]{:S(2)}) copy-start(f32[2]{0:T(128)} %param.13) | copy-start | bytes 28
  232.5 1.9 copy-start.3
  235.1 1.3 copy-start.4
  249.7 47.9 %all-to-all-start.1 = ((f32[16,1,2,16384]{3,1,2,0:T(1,128)}), f32[16,1,2,16384]{3,1,2,0:T(1,128)S(1)}, u32[]{:S(2)}, u32[]{:S(2)}) async-start(f32[16,1,2,16384]{3,1,2,0:T(1,128)} %bitcast.319), calls=%async_computation.1 | async-start | bytes 4194304 | tf_op jit(solution)/shard_map/all_to_all | solution.py:203
  481.1 5.1 %copy-start.5 = (f32[1,128,16,128]{3,2,1,0:T(8,128)S(1)}, f32[1,128,16,128]{3,2,1,0:T(8,128)}, u32[]{:S(2)}) copy-start(f32[1,128,16,128]{3,2,1,0:T(8,128)} %fusion.24) | copy-start | bytes 3145732
  483.7 3.7 copy-start.6
  483.7 3.7 copy-start.7
  487.4 1.5 copy-start.8
  487.4 2.3 copy-start.9
Sparse Core Ops, SparseCore 0:
  162.8 34.4 all-gather.2
  199.4 33.0 all-gather.4
where the time goes:
time: 508 us; the launch traced here: 498 us
  waiting for transfers between devices  147 us (29%)
  blocking collectives  137 us (27%)
  matrix products  106 us (21%)
  local copies, waits for them, and re-layouts  47.2 us (9%)
  other arithmetic  31.7 us (6%)
  between operations  15.1 us (3%)
  starting transfers between devices  14 us (3%)
    all_to_all x1, blocking collectives, local(): lax.all_to_all(columns_to_sending(stacked, groups, slab, cols_own), 'pix'...  103 us
    all_gather x2, waiting for transfers between devices, entering(): pieces = jax.tree.map(lambda part: lax.all_gather(part, axis), value)  65.5 us
    all_to_all x1, waiting for transfers between devices, local(): lax.all_to_all(sending, 'pix', split_axis=0, concat_axis=0, tiled=True)  41.4 us
    all_to_all x1, waiting for transfers between devices, local(): lax.all_to_all(outgoing, 'pix', split_axis=0, concat_axis=0, tiled=True)  40.2 us
    psum x1, blocking collectives, local(): total = lax.psum(jnp.sum(density, axis=(1, 2)), 'pix')  33.9 us
    dot_general x16, matrix products, deposit_group(): jnp.einsum('grk,gkc->grc', row_hot, col_hot, preferred_element_type=jnp.f...  21.1 us
    select_n x16, other arithmetic, deposit_group(): tile_cols = cell_ids % TC  11.7 us
    select_n x16, other arithmetic, deposit_group(): tile_rows = cell_ids // TC  11.7 us
  transfers between devices with their start and end apart: 4, of which 4 were waited for; matrix products, arithmetic and copies ran while one was open for 1% of the time, Pallas kernels for 0%

commit v1 on v0

--- a/solution.py
+++ b/solution.py
@@ -4,7 +4,10 @@
 import jax
 import jax.numpy as jnp
 from jax import lax
+from jax.experimental import pallas as pl
+from jax.experimental.pallas import tpu as pltpu
 from jax.sharding import PartitionSpec as P
+import numpy as np
 
 L = 2048
 TR = 16
@@ -221,6 +224,390 @@
     return (convergence, shear_one * scale, shear_two * scale)
 
 
+INNER = 128
+OUTER = L // INNER
+HALF_BLOCKS = OUTER // 2
+
+
+def block_columns():
+    cols = np.zeros((HALF_BLOCKS, INNER), np.int64)
+    for b in range(HALF_BLOCKS - 1):
+        cols[b] = b + 1 + OUTER * np.arange(INNER)
+    half = np.arange(INNER // 2)
+    cols[-1] = np.concatenate([OUTER * half, HALF_BLOCKS + OUTER * half])
+    return cols
+
+
+def split_table(table):
+    high = table.astype(jnp.bfloat16)
+    low = (table - high.astype(np.float64)).astype(jnp.bfloat16)
+    return high, low
+
+
+def row_tables():
+    n2 = np.arange(INNER)
+    out = np.zeros((HALF_BLOCKS, 2 * INNER, 2 * INNER))
+    cols = block_columns()
+    for b in range(HALF_BLOCKS):
+        angle = 2 * np.pi / L * ((n2[:, None] * cols[b][None, :]) % L)
+        co, si = np.cos(angle), np.sin(angle)
+        if b < HALF_BLOCKS - 1:
+            out[b] = np.block([[co, -si], [si, co]])
+        else:
+            h = INNER // 2
+            out[b, :INNER, :h] = co[:, :h]
+            out[b, :INNER, INNER : INNER + h] = -si[:, :h]
+            out[b, INNER:, h:INNER] = co[:, h:]
+            out[b, INNER:, INNER + h :] = -si[:, h:]
+    return split_table(out)
+
+
+def column_tables():
+    idx = np.arange(INNER)
+    angle = 2 * np.pi / INNER * ((idx[:, None] * idx[None, :]) % INNER)
+    co, si = np.cos(angle), np.sin(angle)
+    return split_table(np.block([[co, si], [-si, co]]))
+
+
+def twiddle_tables():
+    angle = 2 * np.pi / L * (np.arange(OUTER)[:, None] * np.arange(INNER)[None, :])
+    return np.cos(angle).astype(np.float32), (-np.sin(angle)).astype(np.float32)
+
+
+def times_root(value, k, n, sign):
+    re, im = value
+    k = k % n
+    if k == 0:
+        return value
+    if 4 * k == n:
+        return (-im, re) if sign > 0 else (im, -re)
+    angle = 2 * math.pi * k / n
+    c, s = math.cos(angle), sign * math.sin(angle)
+    if 8 * k == n or 8 * k == 3 * n:
+        if c > 0:
+            return ((re - im) * c, (re + im) * c) if sign > 0 else ((re + im) * c, (im - re) * c)
+        c = -c
+        return ((re + im) * -c, (re - im) * c) if sign > 0 else ((im - re) * c, (re + im) * -c)
+    return (re * c - im * s, re * s + im * c)
+
+
+def fft_list(values, sign):
+    n = len(values)
+    if n == 1:
+        return values
+    even = fft_list(values[0::2], sign)
+    odd = fft_list(values[1::2], sign)
+    odd = [times_root(v, k, n, sign) for k, v in enumerate(odd)]
+    return [(a[0] + b[0], a[1] + b[1]) for a, b in zip(even, odd)] + [
+        (a[0] - b[0], a[1] - b[1]) for a, b in zip(even, odd)
+    ]
+
+
+def split_value(value):
+    high = value.astype(jnp.bfloat16)
+    return high, (value - high.astype(jnp.float32)).astype(jnp.bfloat16)
+
+
+def three_pass(left, right, dims):
+    dot = lambda a, b: lax.dot_general(a, b, (dims, ((), ())), preferred_element_type=jnp.float32)
+    return dot(left[0], right[0]) + (dot(left[0], right[1]) + dot(left[1], right[0]))
+
+
+def deposit_kernel(slot_ref, cell_ref, mass_ref, *out_refs):
+    planes, tiles, per_tile = cell_ref.shape
+    groups, rows, _ = out_refs[0].shape
+    cap = rows // TR
+    row_id = lax.broadcasted_iota(jnp.int32, (TR, per_tile), 0)
+    col_id = lax.broadcasted_iota(jnp.int32, (TC, per_tile), 0)
+    for p in range(planes):
+        out_ref = out_refs[p]
+        out_ref[...] = jnp.zeros_like(out_ref)
+        total = jnp.sum(jnp.sum(mass_ref[p].astype(jnp.float32), axis=0, keepdims=True), axis=1, keepdims=True)
+        out_ref[:, cap * TR :, :] = jnp.broadcast_to(total[None], (groups, rows - cap * TR, TC))
+
+        def batch(g, _):
+            base = pl.multiple_of(g * 16, 16)
+            cells = cell_ref[p, pl.ds(base, 16), :]
+            weights = mass_ref[p, pl.ds(base, 16), :].astype(jnp.float32)
+            for i in range(16):
+                cell = cells[i : i + 1]
+                weight = weights[i : i + 1]
+                row_hot = jnp.where(row_id == cell // TC, weight, 0.0).astype(jnp.bfloat16)
+                col_hot = jnp.where(col_id == cell % TC, 1.0, 0.0).astype(jnp.bfloat16)
+                tile = lax.dot_general(
+                    row_hot, col_hot, (((1,), (1,)), ((), ())), preferred_element_type=jnp.float32
+                )
+                slot = slot_ref[p, base + i]
+                out_ref[slot // cap, pl.ds(pl.multiple_of((slot % cap) * TR, TR), TR), :] = tile
+            return 0
+
+        lax.fori_loop(0, tiles // 16, batch, 0)
+
+
+def assemble_kernel(place_ref, in_ref, out_ref, held):
+    groups, rows, _ = in_ref.shape
+    cap = rows // TR
+    tiles = out_ref.shape[0]
+    held[...] = jnp.zeros_like(held)
+    total = in_ref[0, cap * TR : cap * TR + 1, 0:1]
+    for s in range(1, groups):
+        total = total + in_ref[s, cap * TR : cap * TR + 1, 0:1]
+
+    def source(s, _):
+        for c in range(cap):
+            at = place_ref[s * cap + c]
+            held[at] = held[at] + in_ref[s, c * TR : (c + 1) * TR, :]
+        return 0
+
+    lax.fori_loop(0, groups, source, 0)
+    factor = (L * L) / total
+    out_ref[...] = held[0:tiles] * factor[None] - 1.0
+
+
+def row_forward_kernel(mix_ref, near0, near1, far0, far1, high_ref, low_ref, conv_ref, out_ref, held):
+    tile_rows = near0.shape[0] // OUTER
+
+    def chunk(t, _):
+        rows = pl.ds(pl.multiple_of(t * TR, TR), TR)
+        packed = []
+        for n in range(OUTER):
+            at = t * OUTER + n
+            fields = (near0[at], near1[at], far0[at], far1[at])
+            pair = []
+            for i in range(2):
+                value = mix_ref[i, 0] * fields[0]
+                for j in range(1, 4):
+                    value = value + mix_ref[i, j] * fields[j]
+                conv_ref[i, rows, n * INNER : (n + 1) * INNER] = value
+                pair.append(value)
+            packed.append(tuple(pair))
+        z = fft_list(packed, -1)
+        for k in range(1, HALF_BLOCKS):
+            (ar, ai), (br, bi) = z[k], z[OUTER - k]
+            held[k - 1, 0, rows, :INNER] = 0.5 * (ar + br)
+            held[k - 1, 0, rows, INNER:] = 0.5 * (ai - bi)
+            held[k - 1, 1, rows, :INNER] = 0.5 * (ai + bi)
+            held[k - 1, 1, rows, INNER:] = 0.5 * (br - ar)
+        for p in range(2):
+            held[HALF_BLOCKS - 1, p, rows, :INNER] = z[0][p]
+            held[HALF_BLOCKS - 1, p, rows, INNER:] = z[HALF_BLOCKS][p]
+        return 0
+
+    lax.fori_loop(0, tile_rows, chunk, 0)
+
+    def block(b, _):
+        slab = tile_rows * TR
+        value = held[b].reshape(2 * slab, 2 * INNER)
+        result = three_pass(split_value(value), (high_ref[b], low_ref[b]), ((1,), (0,)))
+        for p in range(2):
+            for half in range(2):
+                out_ref[b, p, half] = result[
+                    p * slab : (p + 1) * slab, half * INNER : (half + 1) * INNER
+                ]
+        return 0
+
+    lax.fori_loop(0, HALF_BLOCKS, block, 0)
+
+
+def column_kernel(in_ref, col_ref, twr_ref, twi_ref, high_ref, low_ref, back_high_ref, back_low_ref, out_ref, held, *back):
+    def twist_of(k, rows):
+        return twr_ref[k, rows, :], twi_ref[k, rows, :]
+
+    def forward(t, _):
+        rows = pl.ds(pl.multiple_of(t * 8, 8), 8)
+        z = fft_list([(in_ref[n, 0, rows, :], in_ref[n, 1, rows, :]) for n in range(OUTER)], -1)
+        for k in range(OUTER):
+            re, im = z[k]
+            if k:
+                c, s = twist_of(k, rows)
+                re, im = re * c - im * s, re * s + im * c
+            held[k, 0, rows, :] = re
+            held[k, 1, rows, :] = im
+        return 0
+
+    lax.fori_loop(0, INNER // 8, forward, 0)
+    signed_v = col_ref[0:1]
+    weight = col_ref[1:2]
+    inner_id = lax.broadcasted_iota(jnp.int32, (INNER, INNER), 0)
+
+    def middle(k, _):
+        value = held[k].reshape(2 * INNER, INNER)
+        spectrum = three_pass((high_ref[...], low_ref[...]), split_value(value), ((1,), (0,)))
+        u = k + OUTER * inner_id
+        signed_u = jnp.where(u >= L // 2, u - L, u).astype(jnp.float32)
+        scale = jnp.where(u == L // 2, 0.0, weight)
+        uu, vv = signed_u * signed_u, signed_v * signed_v
+        over = scale / jnp.maximum(uu + vv, 1.0)
+        kernels = ((vv - uu) * over, 2.0 * signed_v * signed_u * over)
+        for f in range(2):
+            twice = jnp.concatenate([kernels[f], kernels[f]], axis=0)
+            result = three_pass(
+                (back_high_ref[...], back_low_ref[...]), split_value(spectrum * twice), ((1,), (0,))
+            )
+            re, im = result[:INNER], result[INNER:]
+            c, s = twr_ref[k], twi_ref[k]
+            back[f][k, 0] = re * c + im * s
+            back[f][k, 1] = im * c - re * s
+        return 0
+
+    lax.fori_loop(0, OUTER, middle, 0)
+    for f in range(2):
+
+        def inverse(t, _):
+            rows = pl.ds(pl.multiple_of(t * 8, 8), 8)
+            x = fft_list([(back[f][k, 0, rows, :], back[f][k, 1, rows, :]) for k in range(OUTER)], 1)
+            for n in range(OUTER):
+                out_ref[n, f, 0, rows, :] = x[n][0]
+                out_ref[n, f, 1, rows, :] = x[n][1]
+            return 0
+
+        lax.fori_loop(0, INNER // 8, inverse, 0)
+
+
+def row_inverse_kernel(in_ref, high_ref, low_ref, one_ref, two_ref, held):
+    slab = in_ref.shape[4]
+    for f, out_ref in enumerate((one_ref, two_ref)):
+
+        def block(b, _):
+            value = jnp.concatenate(
+                [jnp.concatenate([in_ref[b, p, f, 0], in_ref[b, p, f, 1]], axis=1) for p in range(2)], axis=0
+            )
+            held[b] = three_pass(split_value(value), (high_ref[b], low_ref[b]), ((1,), (1,))).reshape(
+                2, slab, 2 * INNER
+            )
+            return 0
+
+        lax.fori_loop(0, HALF_BLOCKS, block, 0)
+
+        def chunk(t, _):
+            rows = pl.ds(pl.multiple_of(t * 8, 8), 8)
+            z = [None] * OUTER
+            last = HALF_BLOCKS - 1
+            z[0] = (held[last, 0, rows, :INNER], held[last, 1, rows, :INNER])
+            z[HALF_BLOCKS] = (held[last, 0, rows, INNER:], held[last, 1, rows, INNER:])
+            for k in range(1, HALF_BLOCKS):
+                ar, ai = held[k - 1, 0, rows, :INNER], held[k - 1, 0, rows, INNER:]
+                br, bi = held[k - 1, 1, rows, :INNER], held[k - 1, 1, rows, INNER:]
+                z[k] = (ar - bi, ai + br)
+                z[OUTER - k] = (ar + bi, br - ai)
+            x = fft_list(z, 1)
+            for n in range(OUTER):
+                for p in range(2):
+                    out_ref[p, rows, n * INNER : (n + 1) * INNER] = x[n][p]
+            return 0
+
+        lax.fori_loop(0, slab // 8, chunk, 0)
+
+
+def call(body, outs, scratch=(), smem=(0,), count=1, megabytes=48, flops=0):
+    space = [
+        pl.BlockSpec(memory_space=pltpu.SMEM if i in smem else pltpu.VMEM) for i in range(count)
+    ]
+    return pl.pallas_call(
+        body,
+        out_shape=outs,
+        in_specs=space,
+        out_specs=jax.tree.map(lambda _: pl.BlockSpec(memory_space=pltpu.VMEM), outs),
+        scratch_shapes=list(scratch),
+        compiler_params=pltpu.CompilerParams(vmem_limit_bytes=megabytes << 20),
+        cost_estimate=pl.CostEstimate(flops=flops, bytes_accessed=4 << 20, transcendentals=0),
+    )
+
+
+def shape(*dims):
+    return jax.ShapeDtypeStruct(dims, jnp.float32)
+
+
+def local_fast(block_tile, cell_index, masses, plane_coef, plane_dist, source_inv):
+    groups = lax.axis_size("pix")
+    me = lax.axis_index("pix")
+    mine_shell = lax.axis_index("shell")
+    planes, local_tiles, per_tile = cell_index.shape
+    slab = L // groups
+    per_owner = slab // TR * (L // TC)
+    cap = max(1, 2 * local_tiles // groups)
+
+    pairs = [(0, 1)]
+    other = lax.ppermute(jnp.concatenate([plane_coef, plane_dist]), "shell", pairs)
+    other_coef = jnp.where(mine_shell > 0, other[:planes], 0.0)
+    other_dist = other[planes:]
+
+    table = block_tile.reshape(planes, groups, local_tiles)
+    owner = table // per_owner
+    earlier = jnp.arange(local_tiles)[:, None] < jnp.arange(local_tiles)[None, :]
+    same_owner = owner[:, :, :, None] == owner[:, :, None, :]
+    rank = jnp.sum(jnp.where(same_owner & earlier[None, None], 1, 0), axis=2)
+    slot = owner * cap + rank
+    my_slots = lax.dynamic_index_in_dim(slot, me, axis=1, keepdims=False)
+    wanted = me * cap + jnp.arange(cap)
+    here = slot[:, :, None, :] == wanted[None, None, :, None]
+    local_index = table - me * per_owner
+    place = jnp.sum(jnp.where(here, local_index[:, :, None, :] + 1, 0), axis=3)
+    place = jnp.where(place > 0, place - 1, per_owner).reshape(planes, groups * cap)
+
+    rows = cap * TR + 8
+    outgoing = call(deposit_kernel, [shape(groups, rows, TC)] * planes, count=3, flops=1 << 29)(
+        my_slots, cell_index, masses
+    )
+    near, far = [], []
+    for p in range(planes):
+        incoming = lax.all_to_all(outgoing[p], "pix", split_axis=0, concat_axis=0, tiled=True)
+        contrast = call(
+            assemble_kernel,
+            shape(per_owner, TR, TC),
+            [pltpu.VMEM((per_owner + 1, TR, TC), jnp.float32)],
+            count=2,
+            flops=1 << 22,
+        )(place[p], incoming)
+        near.append(contrast)
+        far.append(lax.ppermute(contrast, "shell", pairs))
+
+    own = plane_coef[None, :] * (1.0 - source_inv[:, None] * plane_dist[None, :])
+    own = jnp.where(jnp.arange(planes)[None, :] <= jnp.arange(planes)[:, None], own, 0.0)
+    before = other_coef[None, :] * (1.0 - source_inv[:, None] * other_dist[None, :])
+    mix = jnp.concatenate([own, before], axis=1)
+
+    row_high, row_low = row_tables()
+    convergence, sending = call(
+        row_forward_kernel,
+        [shape(planes, slab, L), shape(HALF_BLOCKS, planes, 2, slab, INNER)],
+        [pltpu.VMEM((HALF_BLOCKS, planes, slab, 2 * INNER), jnp.float32)],
+        count=7,
+        flops=1 << 30,
+    )(mix, *near, *far, row_high, row_low)
+    arrived = lax.all_to_all(
+        sending.reshape(groups, 2, slab, INNER), "pix", split_axis=0, concat_axis=0, tiled=True
+    )
+
+    columns = jnp.asarray(block_columns().astype(np.float32))
+    mine = lax.dynamic_index_in_dim(columns, me // planes, axis=0, keepdims=False)
+    special = (me // planes == HALF_BLOCKS - 1) & (mine > 0)
+    weight = jnp.where(special, 2.0, 1.0) / (L * L)
+    signed = jnp.where(mine >= L // 2, mine - L, mine)
+    col_info = jnp.stack([signed, weight])
+    col_high, col_low = column_tables()
+    tw_real, tw_imag = twiddle_tables()
+    spread = lambda t: jnp.broadcast_to(jnp.asarray(t)[:, :, None], (OUTER, INNER, INNER))
+    leaving = call(
+        column_kernel,
+        shape(groups, 2, 2, slab, INNER),
+        [pltpu.VMEM((OUTER, 2, INNER, INNER), jnp.float32)] * 3,
+        smem=(),
+        count=8,
+        flops=1 << 31,
+    )(arrived, col_info, spread(tw_real), spread(tw_imag), col_high, col_low, col_high.T.copy(), col_low.T.copy())
+    landed = lax.all_to_all(leaving, "pix", split_axis=0, concat_axis=0, tiled=True)
+    shear_one, shear_two = call(
+        row_inverse_kernel,
+        [shape(planes, slab, L)] * 2,
+        [pltpu.VMEM((HALF_BLOCKS, planes, slab, 2 * INNER), jnp.float32)],
+        smem=(),
+        count=3,
+        flops=1 << 31,
+    )(landed.reshape(HALF_BLOCKS, planes, 2, 2, slab, INNER), row_high, row_low)
+    return convergence, shear_one, shear_two
+
+
 def solution(mesh):
     placed = (
         P("shell", None),
@@ -230,8 +617,19 @@
         P("shell"),
         P("shell"),
     )
+    shells, groups = mesh.shape["shell"], mesh.shape["pix"]
+
+    def body(block_tile, cell_index, *rest):
+        fits = (
+            shells == 2
+            and cell_index.shape[0] == 2
+            and groups == OUTER
+            and cell_index.shape[1] % 16 == 0
+        )
+        return (local_fast if fits else local)(block_tile, cell_index, *rest)
+
     return jax.shard_map(
-        local,
+        body,
         mesh=mesh,
         in_specs=placed,
         out_specs=(P("shell", "pix", None), P("shell", "pix", None), P("shell", "pix", None)),

time: 508 us -> 288 us (0.57); the launches traced: 498 us -> 287 us
  matrix products: 106 us -> 0 us
  waiting for transfers between devices: 147 us -> 80.1 us
  local copies, waits for them, and re-layouts: 47.2 us -> 4.75 us
  Pallas kernels: 0 us -> 40 us
  other arithmetic: 31.7 us -> 2.23 us
  between operations: 15.1 us -> 0.9 us
  starting transfers between devices: 14 us -> 19.8 us
    dot_general x67 -> x0, matrix products: 106 us -> none  [the longest x16 21.1 us: deposit_group(): jnp.einsum('grk,gkc->grc', row_hot, col_hot, preferred_element_type=jnp.f...]
    all_gather x2 -> x0, waiting for transfers between devices: 65.5 us -> none  [entering(): pieces = jax.tree.map(lambda part: lax.all_gather(part, axis), value)]
    pallas_call x0 -> x6, Pallas kernels: none -> 40 us  [the longest x1 13.7 us: local_fast(): call(column_kernel, shape(groups, 2, 2, slab, INNER), [pltpu.VMEM((OUTER,...]
    all_to_all x1 -> x2, blocking collectives: 103 us -> 139 us  [the longest x1 104 us: local_fast(): lax.all_to_all(leaving, 'pix', split_axis=0, concat_axis=0, tiled=True)]
    psum x1 -> x0, blocking collectives: 33.9 us -> none  [local(): total = lax.psum(jnp.sum(density, axis=(1, 2)), 'pix')]
    all_to_all x2, waiting for transfers between devices: 81.6 us -> 58.7 us  [the longest x1 40.7 us: local_fast(): lax.all_to_all(sending.reshape(groups, 2, slab, INNER), 'pix', split_axis...]
    select_n x32 -> x5, other arithmetic: 23.4 us -> 0.97 us  [the longest x1 0.8 us: local_fast(): signed = jnp.where(mine >= L // 2, mine - L, mine)]
    ppermute x0 -> x3, waiting for transfers between devices: none -> 21.4 us  [the longest x1 21.4 us: local_fast(): lax.ppermute(jnp.concatenate([plane_coef, plane_dist]), 'shell', pairs)]
  transfers between devices with their start and end apart: 4 -> 5, of which waited for: 4 -> 3; matrix products, arithmetic and copies ran while one was open for 1% -> 1% of each run, Pallas kernels for 0% -> 1%
where the time goes in v1:
time: 288 us; the launch traced here: 287 us
  blocking collectives  139 us (48%)
  waiting for transfers between devices  80.1 us (28%)
  Pallas kernels  40 us (14%)
  starting transfers between devices  19.8 us (7%)
  local copies, waits for them, and re-layouts  4.75 us (2%)
    all_to_all x1, blocking collectives, local_fast(): lax.all_to_all(leaving, 'pix', split_axis=0, concat_axis=0, tiled=True)  104 us
    all_to_all x1, waiting for transfers between devices, local_fast(): lax.all_to_all(sending.reshape(groups, 2, slab, INNER), 'pix', split_axis...  40.7 us
    all_to_all x1, blocking collectives, local_fast(): lax.all_to_all(outgoing[p], 'pix', split_axis=0, concat_axis=0, tiled=True)  35.3 us
    ppermute x1, waiting for transfers between devices, local_fast(): lax.ppermute(jnp.concatenate([plane_coef, plane_dist]), 'shell', pairs)  21.4 us
    all_to_all x1, waiting for transfers between devices, local_fast(): lax.all_to_all(outgoing[p], 'pix', split_axis=0, concat_axis=0, tiled=True)  18 us
    pallas_call x1, Pallas kernels, local_fast(): call(column_kernel, shape(groups, 2, 2, slab, INNER), [pltpu.VMEM((OUTER,...  13.7 us
    pallas_call x1, Pallas kernels, local_fast(): call(row_inverse_kernel, [shape(planes, slab, L)] * 2, [pltpu.VMEM((HALF_...  10.2 us
    ppermute x2, starting transfers between devices, local_fast(): far.append(lax.ppermute(contrast, 'shell', pairs))  7.38 us
  transfers between devices with their start and end apart: 5, of which 3 were waited for; matrix products, arithmetic and copies ran while one was open for 1% of the time, Pallas kernels for 1%

profile of v1, /device:TPU:1, one launch (start us, length us, event | category | flops | bytes accessed | tf_op | source)
XLA Modules:
  0.0 286.6 jit_solution(4398044963441686869)
XLA Ops:
  0.7 0.8 reshape.119
  1.5 0.4 select_reduce_fusion
  1.9 0.9 copy-done.7
  2.8 0.9 copy-done.8
  3.7 7.0 %shard_map.166 = (f32[16,136,128]{2,1,0:T(8,128)}, f32[16,136,128]{2,1,0:T(8,128)S(1)}) custom-call(s32[2,64]{1,0:T(2,128)S(1)} %bitcast.3, s32[2,64,512]{2,1,0:T(8,128)S(1)} %copy-done.7, bf16[2,64,512]{2,1,0:T(8,128)(2,1)S(1)} %copy-done.8), custom_call_target="tpu_custom_call" | custom-call | flops 536870912 | bytes 4194304 | tf_op jit(solution)/shard_map/pallas_call | solution.py:549
  10.7 35.3 %all_to_all.20.in_ref = f32[16,136,128]{2,1,0:T(8,128)S(1)} all-to-all(f32[16,136,128]{2,1,0:T(8,128)S(1)} %get-tuple-element.10), channel_id=1, replica_groups=mesh['shell'=2,'pix'=16] {'pix'}, dimensions={0} | all-to-all | bytes 2228224 | tf_op jit(solution)/shard_map/all_to_all | solution.py:554
  46.0 3.9 %all-to-all-start = ((f32[16,136,128]{2,1,0:T(8,128)}), f32[16,136,128]{2,1,0:T(8,128)S(1)}, u32[]{:S(2)}, u32[]{:S(2)}) async-start(f32[16,136,128]{2,1,0:T(8,128)} %get-tuple-element.9), calls=%async_computation | async-start | bytes 2228224 | tf_op jit(solution)/shard_map/all_to_all | solution.py:554
  49.9 0.7 select_reduce_fusion.1
  50.6 0.1 squeeze.14.place_ref
  50.7 0.1 squeeze.12.place_ref
  50.8 1.3 shard_map.168.near1
  52.1 4.1 %collective-permute-start.2 = (f32[128,16,128]{2,1,0:T(8,128)S(1)}, f32[128,16,128]{2,1,0:T(8,128)}, u32[]{:S(2)}, u32[]{:S(2)}) collective-permute-start(f32[128,16,128]{2,1,0:T(8,128)S(1)} %shard_map.168.near1), channel_id=1, source_target_pairs={{0,16},{1,17},{2,18},{3,19},{4,20},{5,21},{6,22},{7,23},{8,24},{9,... | collective-permute-start | bytes 3145736 | tf_op jit(solution)/shard_map/ppermute | solution.py:563
  56.3 18.0 %all-to-all-done.in_ref = f32[16,136,128]{2,1,0:T(8,128)S(1)} async-done(((f32[16,136,128]{2,1,0:T(8,128)}), f32[16,136,128]{2,1,0:T(8,128)S(1)}, u32[]{:S(2)}, u32[]{:S(2)}) %all-to-all-start) | async-done | bytes 1114144 | tf_op jit(solution)/shard_map/all_to_all | solution.py:554
  74.3 1.3 shard_map.167.near0
  75.6 3.2 %collective-permute-start.1 = (f32[128,16,128]{2,1,0:T(8,128)S(1)}, f32[128,16,128]{2,1,0:T(8,128)S(1)}, u32[]{:S(2)}, u32[]{:S(2)}) collective-permute-start(f32[128,16,128]{2,1,0:T(8,128)S(1)} %shard_map.167.near0), channel_id=1, source_target_pairs={{0,16},{1,17},{2,18},{3,19},{4,20},{5,21},{6,22},{7,23},{8,24},{9,... | collective-permute-start | bytes 3145736 | tf_op jit(solution)/shard_map/ppermute | solution.py:563
  78.9 0.1 pad_maximum_fusion.2
  78.9 1.3 collective-permute-start
  80.2 21.4 %collective-permute-done = f32[4]{0:T(128)S(1)} collective-permute-done((f32[4]{0:T(128)S(1)}, f32[4]{0:T(128)S(1)}, u32[]{:S(2)}, u32[]{:S(2)}) %collective-permute-start) | collective-permute-done | bytes 48 | tf_op jit(solution)/shard_map/ppermute | solution.py:531
  101.6 0.1 broadcast_select_fusion
  101.7 0.1 compare_select_fusion.1
  101.8 0.1 pad_maximum_fusion.mix_ref
  101.9 1.2 copy-done.1
  103.1 6.6 %shard_map.169 = (f32[2,128,2048]{2,1,0:T(8,128)}, f32[8,2,2,128,128]{4,3,2,1,0:T(8,128)}) custom-call(f32[2,4]{1,0:T(2,128)S(1)} %pad_maximum_fusion.mix_ref, f32[128,16,128]{2,1,0:T(8,128)S(1)} %shard_map.167.near0, f32[128,16,128]{2,1,0:T(8,128)S(1)} %shard_map.168.near1, f32[128,16,128]{2,1,0:T(8,128)S(1)} %collective-permute-done.1.far0, ...), custom_call_target="tpu_custom_call" | custom-call | flops 1073741824 | bytes 4194304 | tf_op jit(solution)/shard_map/pallas_call | solution.py:571
  109.7 7.2 %all-to-all-start.2 = ((f32[16,2,128,128]{3,2,1,0:T(8,128)}), f32[16,2,128,128]{3,2,1,0:T(8,128)S(1)}, u32[]{:S(2)}, u32[]{:S(2)}) async-start(f32[16,2,128,128]{3,2,1,0:T(8,128)} %bitcast.5), calls=%async_computation.2 | async-start | bytes 4194304 | tf_op jit(solution)/shard_map/all_to_all | solution.py:578
  116.9 0.0 copy-start.4
  116.9 0.8 compare_select_fusion
  117.8 40.7 %all-to-all-done.2.in_ref = f32[16,2,128,128]{3,2,1,0:T(8,128)S(1)} async-done(((f32[16,2,128,128]{3,2,1,0:T(8,128)}), f32[16,2,128,128]{3,2,1,0:T(8,128)S(1)}, u32[]{:S(2)}, u32[]{:S(2)}) %all-to-all-start.2) | async-done | bytes 2097184 | tf_op jit(solution)/shard_map/all_to_all | solution.py:578
  158.4 0.3 broadcast_in_dim.77.twr_ref
  158.8 0.3 broadcast_in_dim.78.twi_ref
  159.1 13.7 %shard_map.170 = f32[16,2,2,128,128]{4,3,2,1,0:T(8,128)} custom-call(f32[16,2,128,128]{3,2,1,0:T(8,128)S(1)} %all-to-all-done.2.in_ref, f32[2,128]{1,0:T(2,128)S(1)} %pad_maximum_fusion.1.col_ref, f32[16,128,128]{2,1,0:T(8,128)S(1)} %broadcast_in_dim.77.twr_ref, f32[16,128,128]{2,1,0:T(8,128)S(1)} %broadcast_in_dim.78.twi_ref, ...), custom_call_target="tpu_custom_call" | custom-call | flops 2147483648 | bytes 4194304 | tf_op jit(solution)/shard_map/pallas_call | solution.py:591
  172.8 103.5 %all_to_all.21 = f32[16,2,2,128,128]{4,3,2,1,0:T(8,128)} all-to-all(f32[16,2,2,128,128]{4,3,2,1,0:T(8,128)} %shard_map.170), channel_id=1, replica_groups=mesh['shell'=2,'pix'=16] {'pix'}, dimensions={0} | all-to-all | bytes 8388608 | tf_op jit(solution)/shard_map/all_to_all | solution.py:599
  276.4 10.2 %shard_map.171 = (f32[2,128,2048]{2,1,0:T(8,128)}, f32[2,128,2048]{2,1,0:T(8,128)}) custom-call(f32[8,2,2,2,128,128]{5,4,3,2,1,0:T(8,128)} %bitcast.4, bf16[8,256,256]{2,1,0:T(8,128)(2,1)S(1)} %copy-done.2, bf16[8,256,256]{2,1,0:T(8,128)(2,1)S(1)} %copy-done), custom_call_target="tpu_custom_call" | custom-call | flops 2147483648 | bytes 4194304 | tf_op jit(solution)/shard_map/pallas_call | solution.py:600
  (34 shorter events, 0.1 us)
Async XLA Ops:
  1.9 1.0 copy-start.7
  2.8 0.9 copy-start.8
  46.0 28.3 %all-to-all-start = ((f32[16,136,128]{2,1,0:T(8,128)}), f32[16,136,128]{2,1,0:T(8,128)S(1)}, u32[]{:S(2)}, u32[]{:S(2)}) async-start(f32[16,136,128]{2,1,0:T(8,128)} %get-tuple-element.9), calls=%async_computation | async-start | bytes 2228224 | tf_op jit(solution)/shard_map/all_to_all | solution.py:554
  50.8 28.1 %copy-start.11 = (f32[2]{0:T(128)S(1)}, f32[2]{0:T(128)}, u32[]{:S(2)}) copy-start(f32[2]{0:T(128)} %param.19) | copy-start | bytes 28
  50.8 28.1 %copy-start.12 = (f32[2]{0:T(128)S(1)}, f32[2]{0:T(128)}, u32[]{:S(2)}) copy-start(f32[2]{0:T(128)} %param.18) | copy-start | bytes 28
  50.8 50.9 %copy-start.13 = (f32[2]{0:T(128)S(1)}, f32[2]{0:T(128)}, u32[]{:S(2)}) copy-start(f32[2]{0:T(128)} %param.20) | copy-start | bytes 28
  52.1 49.8 %collective-permute-start.2 = (f32[128,16,128]{2,1,0:T(8,128)S(1)}, f32[128,16,128]{2,1,0:T(8,128)}, u32[]{:S(2)}, u32[]{:S(2)}) collective-permute-start(f32[128,16,128]{2,1,0:T(8,128)S(1)} %shard_map.168.near1), channel_id=1, source_target_pairs={{0,16},{1,17},{2,18},{3,19},{4,20},{5,21},{6,22},{7,23},{8,24},{9,... | collective-permute-start | bytes 3145736 | tf_op jit(solution)/shard_map/ppermute | solution.py:563
  75.6 26.3 %collective-permute-start.1 = (f32[128,16,128]{2,1,0:T(8,128)S(1)}, f32[128,16,128]{2,1,0:T(8,128)S(1)}, u32[]{:S(2)}, u32[]{:S(2)}) collective-permute-start(f32[128,16,128]{2,1,0:T(8,128)S(1)} %shard_map.167.near0), channel_id=1, source_target_pairs={{0,16},{1,17},{2,18},{3,19},{4,20},{5,21},{6,22},{7,23},{8,24},{9,... | collective-permute-start | bytes 3145736 | tf_op jit(solution)/shard_map/ppermute | solution.py:563
  78.9 22.7 %collective-permute-start = (f32[4]{0:T(128)S(1)}, f32[4]{0:T(128)S(1)}, u32[]{:S(2)}, u32[]{:S(2)}) collective-permute-start(f32[4]{0:T(128)S(1)} %pad_maximum_fusion.2), channel_id=1, source_target_pairs={{0,16},{1,17},{2,18},{3,19},{4,20},{5,21},{6,22},{7,23},{8,24},{9,... | collective-permute-start | bytes 56 | tf_op jit(solution)/shard_map/ppermute | solution.py:531
  101.9 1.2 copy-start.1
  109.7 48.8 %copy-start.10 = (f32[16,128]{1,0:T(8,128)S(1)}, f32[16,128]{1,0:T(8,128)}, u32[]{:S(2)}) copy-start(f32[16,128]{1,0:T(8,128)} %constant.95.clone) | copy-start | bytes 24580
  109.7 49.1 %copy-start.9 = (f32[16,128]{1,0:T(8,128)S(1)}, f32[16,128]{1,0:T(8,128)}, u32[]{:S(2)}) copy-start(f32[16,128]{1,0:T(8,128)} %constant.96.clone) | copy-start | bytes 24580
  109.7 48.7 %all-to-all-start.2 = ((f32[16,2,128,128]{3,2,1,0:T(8,128)}), f32[16,2,128,128]{3,2,1,0:T(8,128)S(1)}, u32[]{:S(2)}, u32[]{:S(2)}) async-start(f32[16,2,128,128]{3,2,1,0:T(8,128)} %bitcast.5), calls=%async_computation.2 | async-start | bytes 4194304 | tf_op jit(solution)/shard_map/all_to_all | solution.py:578
  116.9 42.2 %copy-start.3 = (bf16[256,256]{1,0:T(8,128)(2,1)S(1)}, bf16[256,256]{1,0:T(8,128)(2,1)}, u32[]{:S(2)}) copy-start(bf16[256,256]{1,0:T(8,128)(2,1)} %constant.100.clone.back_low_ref) | copy-start | bytes 393220
  116.9 42.2 %copy-start.4 = (bf16[256,256]{1,0:T(8,128)(2,1)S(1)}, bf16[256,256]{1,0:T(8,128)(2,1)}, u32[]{:S(2)}) copy-start(bf16[256,256]{1,0:T(8,128)(2,1)} %constant.99.clone.back_high_ref) | copy-start | bytes 393220
  116.9 42.2 %copy-start.5 = (bf16[256,256]{1,0:T(8,128)(2,1)S(1)}, bf16[256,256]{1,0:T(8,128)(2,1)}, u32[]{:S(2)}) copy-start(bf16[256,256]{1,0:T(8,128)(2,1)} %constant.98.clone.low_ref) | copy-start | bytes 393220
  116.9 42.2 %copy-start.6 = (bf16[256,256]{1,0:T(8,128)(2,1)S(1)}, bf16[256,256]{1,0:T(8,128)(2,1)}, u32[]{:S(2)}) copy-start(bf16[256,256]{1,0:T(8,128)(2,1)} %constant.97.clone.high_ref) | copy-start | bytes 393220
  172.8 103.5 %copy-start = (bf16[8,256,256]{2,1,0:T(8,128)(2,1)S(1)}, bf16[8,256,256]{2,1,0:T(8,128)(2,1)}, u32[]{:S(2)}) copy-start(bf16[8,256,256]{2,1,0:T(8,128)(2,1)} %constant.93.clone.low_ref) | copy-start | bytes 3145732
  172.8 103.5 %copy-start.2 = (bf16[8,256,256]{2,1,0:T(8,128)(2,1)S(1)}, bf16[8,256,256]{2,1,0:T(8,128)(2,1)}, u32[]{:S(2)}) copy-start(bf16[8,256,256]{2,1,0:T(8,128)(2,1)} %constant.92.clone.high_ref) | copy-start | bytes 3145732

commit v2 on v1

--- a/solution.py
+++ b/solution.py
@@ -409,94 +409,106 @@
     lax.fori_loop(0, HALF_BLOCKS, block, 0)
 
 
-def column_kernel(in_ref, col_ref, twr_ref, twi_ref, high_ref, low_ref, back_high_ref, back_low_ref, out_ref, held, *back):
-    def twist_of(k, rows):
-        return twr_ref[k, rows, :], twi_ref[k, rows, :]
-
+def column_inverse(f, col_ref, twr_ref, twi_ref, spectrum_of, back_high_ref, back_low_ref, out_ref, back):
+    signed_v = col_ref[0:1]
+    weight = col_ref[1:2]
+    inner_id = lax.broadcasted_iota(jnp.int32, (INNER, INNER), 0)
+
+    def middle(k, _):
+        spectrum = spectrum_of(k)
+        u = k + OUTER * inner_id
+        signed_u = jnp.where(u >= L // 2, u - L, u).astype(jnp.float32)
+        scale = jnp.where(u == L // 2, 0.0, weight)
+        uu, vv = signed_u * signed_u, signed_v * signed_v
+        over = scale / jnp.maximum(uu + vv, 1.0)
+        kernel = (vv - uu) * over if f == 0 else 2.0 * signed_v * signed_u * over
+        twice = jnp.concatenate([kernel, kernel], axis=0)
+        result = three_pass(
+            (back_high_ref[...], back_low_ref[...]), split_value(spectrum * twice), ((1,), (0,))
+        )
+        re, im = result[:INNER], result[INNER:]
+        c, s = twr_ref[k], twi_ref[k]
+        back[k, 0] = re * c + im * s
+        back[k, 1] = im * c - re * s
+        return 0
+
+    lax.fori_loop(0, OUTER, middle, 0)
+
+    def inverse(t, _):
+        rows = pl.ds(pl.multiple_of(t * 8, 8), 8)
+        x = fft_list([(back[k, 0, rows, :], back[k, 1, rows, :]) for k in range(OUTER)], 1)
+        for n in range(OUTER):
+            out_ref[n, 0, rows, :] = x[n][0]
+            out_ref[n, 1, rows, :] = x[n][1]
+        return 0
+
+    lax.fori_loop(0, INNER // 8, inverse, 0)
+
+
+def column_first_kernel(
+    in_ref, col_ref, twr_ref, twi_ref, high_ref, low_ref, back_high_ref, back_low_ref, out_ref, spec_ref, held, back
+):
     def forward(t, _):
         rows = pl.ds(pl.multiple_of(t * 8, 8), 8)
         z = fft_list([(in_ref[n, 0, rows, :], in_ref[n, 1, rows, :]) for n in range(OUTER)], -1)
         for k in range(OUTER):
             re, im = z[k]
             if k:
-                c, s = twist_of(k, rows)
+                c, s = twr_ref[k, rows, :], twi_ref[k, rows, :]
                 re, im = re * c - im * s, re * s + im * c
             held[k, 0, rows, :] = re
             held[k, 1, rows, :] = im
         return 0
 
     lax.fori_loop(0, INNER // 8, forward, 0)
-    signed_v = col_ref[0:1]
-    weight = col_ref[1:2]
-    inner_id = lax.broadcasted_iota(jnp.int32, (INNER, INNER), 0)
-
-    def middle(k, _):
+
+    def spectrum_of(k):
         value = held[k].reshape(2 * INNER, INNER)
         spectrum = three_pass((high_ref[...], low_ref[...]), split_value(value), ((1,), (0,)))
-        u = k + OUTER * inner_id
-        signed_u = jnp.where(u >= L // 2, u - L, u).astype(jnp.float32)
-        scale = jnp.where(u == L // 2, 0.0, weight)
-        uu, vv = signed_u * signed_u, signed_v * signed_v
-        over = scale / jnp.maximum(uu + vv, 1.0)
-        kernels = ((vv - uu) * over, 2.0 * signed_v * signed_u * over)
-        for f in range(2):
-            twice = jnp.concatenate([kernels[f], kernels[f]], axis=0)
-            result = three_pass(
-                (back_high_ref[...], back_low_ref[...]), split_value(spectrum * twice), ((1,), (0,))
-            )
-            re, im = result[:INNER], result[INNER:]
-            c, s = twr_ref[k], twi_ref[k]
-            back[f][k, 0] = re * c + im * s
-            back[f][k, 1] = im * c - re * s
-        return 0
-
-    lax.fori_loop(0, OUTER, middle, 0)
-    for f in range(2):
-
-        def inverse(t, _):
-            rows = pl.ds(pl.multiple_of(t * 8, 8), 8)
-            x = fft_list([(back[f][k, 0, rows, :], back[f][k, 1, rows, :]) for k in range(OUTER)], 1)
-            for n in range(OUTER):
-                out_ref[n, f, 0, rows, :] = x[n][0]
-                out_ref[n, f, 1, rows, :] = x[n][1]
-            return 0
-
-        lax.fori_loop(0, INNER // 8, inverse, 0)
-
-
-def row_inverse_kernel(in_ref, high_ref, low_ref, one_ref, two_ref, held):
-    slab = in_ref.shape[4]
-    for f, out_ref in enumerate((one_ref, two_ref)):
-
-        def block(b, _):
-            value = jnp.concatenate(
-                [jnp.concatenate([in_ref[b, p, f, 0], in_ref[b, p, f, 1]], axis=1) for p in range(2)], axis=0
-            )
-            held[b] = three_pass(split_value(value), (high_ref[b], low_ref[b]), ((1,), (1,))).reshape(
-                2, slab, 2 * INNER
-            )
-            return 0
-
-        lax.fori_loop(0, HALF_BLOCKS, block, 0)
-
-        def chunk(t, _):
-            rows = pl.ds(pl.multiple_of(t * 8, 8), 8)
-            z = [None] * OUTER
-            last = HALF_BLOCKS - 1
-            z[0] = (held[last, 0, rows, :INNER], held[last, 1, rows, :INNER])
-            z[HALF_BLOCKS] = (held[last, 0, rows, INNER:], held[last, 1, rows, INNER:])
-            for k in range(1, HALF_BLOCKS):
-                ar, ai = held[k - 1, 0, rows, :INNER], held[k - 1, 0, rows, INNER:]
-                br, bi = held[k - 1, 1, rows, :INNER], held[k - 1, 1, rows, INNER:]
-                z[k] = (ar - bi, ai + br)
-                z[OUTER - k] = (ar + bi, br - ai)
-            x = fft_list(z, 1)
-            for n in range(OUTER):
-                for p in range(2):
-                    out_ref[p, rows, n * INNER : (n + 1) * INNER] = x[n][p]
-            return 0
-
-        lax.fori_loop(0, slab // 8, chunk, 0)
+        spec_ref[k] = spectrum
+        return spectrum
+
+    column_inverse(0, col_ref, twr_ref, twi_ref, spectrum_of, back_high_ref, back_low_ref, out_ref, back)
+
+
+def column_second_kernel(spec_ref, col_ref, twr_ref, twi_ref, back_high_ref, back_low_ref, out_ref, back):
+    column_inverse(
+        1, col_ref, twr_ref, twi_ref, lambda k: spec_ref[k], back_high_ref, back_low_ref, out_ref, back
+    )
+
+
+def row_inverse_kernel(in_ref, high_ref, low_ref, out_ref, held):
+    slab = in_ref.shape[3]
+
+    def block(b, _):
+        value = jnp.concatenate(
+            [jnp.concatenate([in_ref[b, p, 0], in_ref[b, p, 1]], axis=1) for p in range(2)], axis=0
+        )
+        held[b] = three_pass(split_value(value), (high_ref[b], low_ref[b]), ((1,), (1,))).reshape(
+            2, slab, 2 * INNER
+        )
+        return 0
+
+    lax.fori_loop(0, HALF_BLOCKS, block, 0)
+
+    def chunk(t, _):
+        rows = pl.ds(pl.multiple_of(t * 8, 8), 8)
+        z = [None] * OUTER
+        last = HALF_BLOCKS - 1
+        z[0] = (held[last, 0, rows, :INNER], held[last, 1, rows, :INNER])
+        z[HALF_BLOCKS] = (held[last, 0, rows, INNER:], held[last, 1, rows, INNER:])
+        for k in range(1, HALF_BLOCKS):
+            ar, ai = held[k - 1, 0, rows, :INNER], held[k - 1, 0, rows, INNER:]
+            br, bi = held[k - 1, 1, rows, :INNER], held[k - 1, 1, rows, INNER:]
+            z[k] = (ar - bi, ai + br)
+            z[OUTER - k] = (ar + bi, br - ai)
+        x = fft_list(z, 1)
+        for n in range(OUTER):
+            for p in range(2):
+                out_ref[p, rows, n * INNER : (n + 1) * INNER] = x[n][p]
+        return 0
+
+    lax.fori_loop(0, slab // 8, chunk, 0)
 
 
 def call(body, outs, scratch=(), smem=(0,), count=1, megabytes=48, flops=0):
@@ -588,23 +600,38 @@
     col_high, col_low = column_tables()
     tw_real, tw_imag = twiddle_tables()
     spread = lambda t: jnp.broadcast_to(jnp.asarray(t)[:, :, None], (OUTER, INNER, INNER))
-    leaving = call(
-        column_kernel,
-        shape(groups, 2, 2, slab, INNER),
-        [pltpu.VMEM((OUTER, 2, INNER, INNER), jnp.float32)] * 3,
+    twiddles = (spread(tw_real), spread(tw_imag))
+    backs = (col_high.T.copy(), col_low.T.copy())
+    work = pltpu.VMEM((OUTER, 2, INNER, INNER), jnp.float32)
+    leaving_one, spectrum = call(
+        column_first_kernel,
+        [shape(groups, 2, slab, INNER), shape(OUTER, 2 * INNER, INNER)],
+        [work, work],
         smem=(),
         count=8,
         flops=1 << 31,
-    )(arrived, col_info, spread(tw_real), spread(tw_imag), col_high, col_low, col_high.T.copy(), col_low.T.copy())
-    landed = lax.all_to_all(leaving, "pix", split_axis=0, concat_axis=0, tiled=True)
-    shear_one, shear_two = call(
+    )(arrived, col_info, *twiddles, col_high, col_low, *backs)
+    landed_one = lax.all_to_all(leaving_one, "pix", split_axis=0, concat_axis=0, tiled=True)
+    leaving_two = call(
+        column_second_kernel,
+        shape(groups, 2, slab, INNER),
+        [work],
+        smem=(),
+        count=6,
+        flops=1 << 31,
+    )(spectrum, col_info, *twiddles, *backs)
+    leaving_two, landed_one = lax.optimization_barrier((leaving_two, landed_one))
+    landed_two = lax.all_to_all(leaving_two, "pix", split_axis=0, concat_axis=0, tiled=True)
+    finish = lambda landed: call(
         row_inverse_kernel,
-        [shape(planes, slab, L)] * 2,
+        shape(planes, slab, L),
         [pltpu.VMEM((HALF_BLOCKS, planes, slab, 2 * INNER), jnp.float32)],
         smem=(),
         count=3,
         flops=1 << 31,
-    )(landed.reshape(HALF_BLOCKS, planes, 2, 2, slab, INNER), row_high, row_low)
+    )(landed.reshape(HALF_BLOCKS, planes, 2, slab, INNER), row_high, row_low)
+    shear_one = finish(landed_one)
+    shear_two = finish(landed_two)
     return convergence, shear_one, shear_two
 
 

time: 288 us -> 292 us (1.014)
  the two profiles are of different devices: /device:TPU:1 before, /device:TPU:15 now
where the time goes in v2:
time: 292 us; the launch traced here: 291 us
  waiting for transfers between devices  174 us (60%)
  Pallas kernels  46 us (16%)
  blocking collectives  32.6 us (11%)
  starting transfers between devices  24.2 us (8%)
  local copies, waits for them, and re-layouts  11 us (4%)
    all_to_all x1, waiting for transfers between devices, local_fast(): lax.all_to_all(sending.reshape(groups, 2, slab, INNER), 'pix', split_axis...  46.6 us
    all_to_all x1, waiting for transfers between devices, local_fast(): lax.all_to_all(leaving_two, 'pix', split_axis=0, concat_axis=0, tiled=True)  41.9 us
    all_to_all x1, waiting for transfers between devices, local_fast(): lax.all_to_all(leaving_one, 'pix', split_axis=0, concat_axis=0, tiled=True)  38 us
    all_to_all x1, blocking collectives, local_fast(): lax.all_to_all(outgoing[p], 'pix', split_axis=0, concat_axis=0, tiled=True)  32.6 us
    ppermute x1, waiting for transfers between devices, local_fast(): lax.ppermute(jnp.concatenate([plane_coef, plane_dist]), 'shell', pairs)  24.2 us
    all_to_all x1, waiting for transfers between devices, local_fast(): lax.all_to_all(outgoing[p], 'pix', split_axis=0, concat_axis=0, tiled=True)  23.1 us
    pallas_call x1, Pallas kernels, local_fast(): call(column_first_kernel, [shape(groups, 2, slab, INNER), shape(OUTER, 2...  13.6 us
    pallas_call x2, Pallas kernels, local_fast(): call(row_inverse_kernel, shape(planes, slab, L), [pltpu.VMEM((HALF_BLOCKS...  10.3 us
  transfers between devices with their start and end apart: 7, of which 5 were waited for; matrix products, arithmetic and copies ran while one was open for 1% of the time, Pallas kernels for 5%

profile of v2, /device:TPU:15, one launch (start us, length us, event | category | flops | bytes accessed | tf_op | source)
XLA Modules:
  0.0 291.1 jit_solution(10525157405388283591)
XLA Ops:
  0.7 0.8 reshape.122
  1.9 0.9 copy-done.9
  2.8 0.9 copy-done.10
  3.7 6.1 %shard_map.166 = (f32[16,136,128]{2,1,0:T(8,128)S(1)}, f32[16,136,128]{2,1,0:T(8,128)S(1)}) custom-call(s32[2,64]{1,0:T(2,128)S(1)} %bitcast.5, s32[2,64,512]{2,1,0:T(8,128)S(1)} %copy-done.9, bf16[2,64,512]{2,1,0:T(8,128)(2,1)S(1)} %copy-done.10), custom_call_target="tpu_custom_call" | custom-call | flops 536870912 | bytes 4194304 | tf_op jit(solution)/shard_map/pallas_call | solution.py:561
  9.8 32.6 %all_to_all.25.in_ref = f32[16,136,128]{2,1,0:T(8,128)S(1)} all-to-all(f32[16,136,128]{2,1,0:T(8,128)S(1)} %get-tuple-element.11), channel_id=1, replica_groups=mesh['shell'=2,'pix'=16] {'pix'}, dimensions={0} | all-to-all | bytes 2228224 | tf_op jit(solution)/shard_map/all_to_all | solution.py:566
  42.5 5.8 %all-to-all-start.1 = ((f32[16,136,128]{2,1,0:T(8,128)}), f32[16,136,128]{2,1,0:T(8,128)S(1)}, u32[]{:S(2)}, u32[]{:S(2)}) async-start(f32[16,136,128]{2,1,0:T(8,128)} %copy-done.2), calls=%async_computation.1 | async-start | bytes 2228224 | tf_op jit(solution)/shard_map/all_to_all | solution.py:566
  48.2 0.7 select_reduce_fusion.1
  49.2 1.3 shard_map.167.near0
  50.5 1.3 collective-permute-start.1
  51.8 23.1 %all-to-all-done.1.in_ref = f32[16,136,128]{2,1,0:T(8,128)S(1)} async-done(((f32[16,136,128]{2,1,0:T(8,128)}), f32[16,136,128]{2,1,0:T(8,128)S(1)}, u32[]{:S(2)}, u32[]{:S(2)}) %all-to-all-start.1) | async-done | bytes 1114144 | tf_op jit(solution)/shard_map/all_to_all | solution.py:566
  74.9 1.4 shard_map.168.near1
  76.3 1.3 collective-permute-start.2
  77.7 1.3 collective-permute-start
  79.0 24.2 %collective-permute-done = f32[4]{0:T(128)S(1)} collective-permute-done((f32[4]{0:T(128)S(1)}, f32[4]{0:T(128)S(1)}, u32[]{:S(2)}, u32[]{:S(2)}) %collective-permute-start) | collective-permute-done | bytes 48 | tf_op jit(solution)/shard_map/ppermute | solution.py:543
  103.4 1.2 copy-done.5
  104.6 6.5 %shard_map.169 = (f32[2,128,2048]{2,1,0:T(8,128)}, f32[8,2,2,128,128]{4,3,2,1,0:T(8,128)}) custom-call(f32[2,4]{1,0:T(2,128)S(1)} %pad_maximum_fusion.mix_ref, f32[128,16,128]{2,1,0:T(8,128)S(1)} %shard_map.167.near0, f32[128,16,128]{2,1,0:T(8,128)S(1)} %shard_map.168.near1, f32[128,16,128]{2,1,0:T(8,128)} %collective-permute-done.1.far0, ...), custom_call_target="tpu_custom_call" | custom-call | flops 1073741824 | bytes 4194304 | tf_op jit(solution)/shard_map/pallas_call | solution.py:583
  111.2 5.1 %all-to-all-start.2 = ((f32[16,2,128,128]{3,2,1,0:T(8,128)}), f32[16,2,128,128]{3,2,1,0:T(8,128)}, u32[]{:S(2)}, u32[]{:S(2)}) async-start(f32[16,2,128,128]{3,2,1,0:T(8,128)} %bitcast.6), calls=%async_computation.2 | async-start | bytes 4194304 | tf_op jit(solution)/shard_map/all_to_all | solution.py:590
  116.3 0.8 compare_select_fusion
  117.1 46.6 %all-to-all-done.2.in_ref = f32[16,2,128,128]{3,2,1,0:T(8,128)} async-done(((f32[16,2,128,128]{3,2,1,0:T(8,128)}), f32[16,2,128,128]{3,2,1,0:T(8,128)}, u32[]{:S(2)}, u32[]{:S(2)}) %all-to-all-start.2) | async-done | bytes 2097184 | tf_op jit(solution)/shard_map/all_to_all | solution.py:590
  164.5 13.6 %shard_map.170 = (f32[16,2,128,128]{3,2,1,0:T(8,128)S(1)}, f32[16,256,128]{2,1,0:T(8,128)}) custom-call(f32[16,2,128,128]{3,2,1,0:T(8,128)} %all-to-all-done.2.in_ref, f32[2,128]{1,0:T(2,128)S(1)} %pad_maximum_fusion.1.col_ref, f32[16,128,128]{2,1,0:T(8,128)S(1)} %broadcast_in_dim.77.twr_ref, f32[16,128,128]{2,1,0:T(8,128)S(1)} %broadcast_in_dim.78.twi_ref, ...), custom_call_target="tpu_custom_call" | custom-call | flops 2147483648 | bytes 4194304 | tf_op jit(solution)/shard_map/pallas_call | solution.py:606
  178.1 1.3 copy-done.1
  179.4 4.8 %all-to-all-start.3 = ((f32[16,2,128,128]{3,2,1,0:T(8,128)}), f32[16,2,128,128]{3,2,1,0:T(8,128)S(1)}, u32[]{:S(2)}, u32[]{:S(2)}) async-start(f32[16,2,128,128]{3,2,1,0:T(8,128)} %copy-done.1), calls=%async_computation.3 | async-start | bytes 4194304 | tf_op jit(solution)/shard_map/all_to_all | solution.py:614
  184.2 1.2 copy-done.4
  185.4 6.8 %shard_map.171 = f32[16,2,128,128]{3,2,1,0:T(8,128)S(1)} custom-call(f32[16,256,128]{2,1,0:T(8,128)} %get-tuple-element.15.spec_ref, f32[2,128]{1,0:T(2,128)S(1)} %pad_maximum_fusion.1.col_ref, f32[16,128,128]{2,1,0:T(8,128)S(1)} %broadcast_in_dim.77.twr_ref, f32[16,128,128]{2,1,0:T(8,128)S(1)} %copy-done.4, bf16[256,256]{1,0:T(8,128)(2,1)S(1)} %copy-done.11, ...), custom_call_target="tpu_custom_call" | custom-call | flops 2147483648 | bytes 4194304 | tf_op jit(solution)/shard_map/pallas_call | solution.py:615
  192.3 1.3 copy-done
  193.6 38.0 %all-to-all-done.3 = f32[16,2,128,128]{3,2,1,0:T(8,128)S(1)} async-done(((f32[16,2,128,128]{3,2,1,0:T(8,128)}), f32[16,2,128,128]{3,2,1,0:T(8,128)S(1)}, u32[]{:S(2)}, u32[]{:S(2)}) %all-to-all-start.3) | async-done | bytes 2097184 | tf_op jit(solution)/shard_map/all_to_all | solution.py:614
  231.6 4.8 %all-to-all-start.4 = ((f32[16,2,128,128]{3,2,1,0:T(8,128)}), f32[16,2,128,128]{3,2,1,0:T(8,128)}, u32[]{:S(2)}, u32[]{:S(2)}) async-start(f32[16,2,128,128]{3,2,1,0:T(8,128)} %copy-done), calls=%async_computation.4 | async-start | bytes 4194304 | tf_op jit(solution)/shard_map/all_to_all | solution.py:624
  236.4 1.2 copy-done.7
  237.7 4.3 %shard_map.172 = f32[2,128,2048]{2,1,0:T(8,128)} custom-call(f32[8,2,2,128,128]{4,3,2,1,0:T(8,128)S(1)} %bitcast.4, bf16[8,256,256]{2,1,0:T(8,128)(2,1)S(1)} %copy-done.6, bf16[8,256,256]{2,1,0:T(8,128)(2,1)S(1)} %copy-done.7), custom_call_target="tpu_custom_call" | custom-call | flops 2147483648 | bytes 4194304 | tf_op jit(solution)/shard_map/pallas_call | solution.py:625
  242.0 41.9 %all-to-all-done.4 = f32[16,2,128,128]{3,2,1,0:T(8,128)} async-done(((f32[16,2,128,128]{3,2,1,0:T(8,128)}), f32[16,2,128,128]{3,2,1,0:T(8,128)}, u32[]{:S(2)}, u32[]{:S(2)}) %all-to-all-start.4) | async-done | bytes 2097184 | tf_op jit(solution)/shard_map/all_to_all | solution.py:624
  283.9 1.2 copy-done.8
  285.2 5.9 %shard_map.173 = f32[2,128,2048]{2,1,0:T(8,128)} custom-call(f32[8,2,2,128,128]{4,3,2,1,0:T(8,128)} %bitcast.3.in_ref, bf16[8,256,256]{2,1,0:T(8,128)(2,1)S(1)} %copy-done.6, bf16[8,256,256]{2,1,0:T(8,128)(2,1)S(1)} %copy-done.8), custom_call_target="tpu_custom_call" | custom-call | flops 2147483648 | bytes 4194304 | tf_op jit(solution)/shard_map/pallas_call | solution.py:625
  (51 shorter events, 1.7 us)
Async XLA Ops:
  1.9 1.0 copy-start.9
  2.8 0.9 copy-start.10
  9.8 32.6 %copy-start.2 = (f32[16,136,128]{2,1,0:T(8,128)}, f32[16,136,128]{2,1,0:T(8,128)S(1)}, u32[]{:S(2)}) copy-start(f32[16,136,128]{2,1,0:T(8,128)S(1)} %get-tuple-element.12) | copy-start | bytes 3342340
  42.5 32.5 %all-to-all-start.1 = ((f32[16,136,128]{2,1,0:T(8,128)}), f32[16,136,128]{2,1,0:T(8,128)S(1)}, u32[]{:S(2)}, u32[]{:S(2)}) async-start(f32[16,136,128]{2,1,0:T(8,128)} %copy-done.2), calls=%async_computation.1 | async-start | bytes 2228224 | tf_op jit(solution)/shard_map/all_to_all | solution.py:566
  49.1 28.5 %copy-start.17 = (f32[2]{0:T(128)S(1)}, f32[2]{0:T(128)}, u32[]{:S(2)}) copy-start(f32[2]{0:T(128)} %param.19) | copy-start | bytes 28
  49.1 28.5 %copy-start.18 = (f32[2]{0:T(128)S(1)}, f32[2]{0:T(128)}, u32[]{:S(2)}) copy-start(f32[2]{0:T(128)} %param.18) | copy-start | bytes 28
  49.2 54.1 %copy-start.19 = (f32[2]{0:T(128)S(1)}, f32[2]{0:T(128)}, u32[]{:S(2)}) copy-start(f32[2]{0:T(128)} %param.20) | copy-start | bytes 28
  50.5 52.9 %collective-permute-start.1 = (f32[128,16,128]{2,1,0:T(8,128)S(1)}, f32[128,16,128]{2,1,0:T(8,128)}, u32[]{:S(2)}, u32[]{:S(2)}) collective-permute-start(f32[128,16,128]{2,1,0:T(8,128)S(1)} %shard_map.167.near0), channel_id=1, source_target_pairs={{0,16},{1,17},{2,18},{3,19},{4,20},{5,21},{6,22},{7,23},{8,24},{9,... | collective-permute-start | bytes 3145736 | tf_op jit(solution)/shard_map/ppermute | solution.py:575
  76.3 27.1 %collective-permute-start.2 = (f32[128,16,128]{2,1,0:T(8,128)S(1)}, f32[128,16,128]{2,1,0:T(8,128)S(1)}, u32[]{:S(2)}, u32[]{:S(2)}) collective-permute-start(f32[128,16,128]{2,1,0:T(8,128)S(1)} %shard_map.168.near1), channel_id=1, source_target_pairs={{0,16},{1,17},{2,18},{3,19},{4,20},{5,21},{6,22},{7,23},{8,24},{9,... | collective-permute-start | bytes 3145736 | tf_op jit(solution)/shard_map/ppermute | solution.py:575
  77.7 25.5 %collective-permute-start = (f32[4]{0:T(128)S(1)}, f32[4]{0:T(128)S(1)}, u32[]{:S(2)}, u32[]{:S(2)}) collective-permute-start(f32[4]{0:T(128)S(1)} %pad_maximum_fusion.2), channel_id=1, source_target_pairs={{0,16},{1,17},{2,18},{3,19},{4,20},{5,21},{6,22},{7,23},{8,24},{9,... | collective-permute-start | bytes 56 | tf_op jit(solution)/shard_map/ppermute | solution.py:543
  103.4 1.2 copy-start.5
  111.2 52.6 %copy-start.16 = (f32[16,128]{1,0:T(8,128)S(1)}, f32[16,128]{1,0:T(8,128)}, u32[]{:S(2)}) copy-start(f32[16,128]{1,0:T(8,128)} %constant.95.clone) | copy-start | bytes 24580
  111.2 52.9 %copy-start.15 = (f32[16,128]{1,0:T(8,128)S(1)}, f32[16,128]{1,0:T(8,128)}, u32[]{:S(2)}) copy-start(f32[16,128]{1,0:T(8,128)} %constant.96.clone) | copy-start | bytes 24580
  111.2 52.6 %all-to-all-start.2 = ((f32[16,2,128,128]{3,2,1,0:T(8,128)}), f32[16,2,128,128]{3,2,1,0:T(8,128)}, u32[]{:S(2)}, u32[]{:S(2)}) async-start(f32[16,2,128,128]{3,2,1,0:T(8,128)} %bitcast.6), calls=%async_computation.2 | async-start | bytes 4194304 | tf_op jit(solution)/shard_map/all_to_all | solution.py:590
  116.3 48.2 %copy-start.11 = (bf16[256,256]{1,0:T(8,128)(2,1)S(1)}, bf16[256,256]{1,0:T(8,128)(2,1)}, u32[]{:S(2)}) copy-start(bf16[256,256]{1,0:T(8,128)(2,1)} %constant.99.clone.back_high_ref) | copy-start | bytes 393220
  116.3 48.2 %copy-start.12 = (bf16[256,256]{1,0:T(8,128)(2,1)S(1)}, bf16[256,256]{1,0:T(8,128)(2,1)}, u32[]{:S(2)}) copy-start(bf16[256,256]{1,0:T(8,128)(2,1)} %constant.100.clone.back_low_ref) | copy-start | bytes 393220
  116.3 48.2 %copy-start.13 = (bf16[256,256]{1,0:T(8,128)(2,1)S(1)}, bf16[256,256]{1,0:T(8,128)(2,1)}, u32[]{:S(2)}) copy-start(bf16[256,256]{1,0:T(8,128)(2,1)} %constant.97.clone.high_ref) | copy-start | bytes 393220
  116.3 48.2 %copy-start.14 = (bf16[256,256]{1,0:T(8,128)(2,1)S(1)}, bf16[256,256]{1,0:T(8,128)(2,1)}, u32[]{:S(2)}) copy-start(bf16[256,256]{1,0:T(8,128)(2,1)} %constant.98.clone.low_ref) | copy-start | bytes 393220
  164.5 13.6 %copy-start.3 = (f32[16,128,128]{2,1,0:T(8,128)}, f32[16,128,128]{2,1,0:T(8,128)S(1)}, u32[]{:S(2)}) copy-start(f32[16,128,128]{2,1,0:T(8,128)S(1)} %broadcast_in_dim.78.twi_ref) | copy-start | bytes 3145732
  178.1 1.3 copy-start.1
  179.4 52.2 %all-to-all-start.3 = ((f32[16,2,128,128]{3,2,1,0:T(8,128)}), f32[16,2,128,128]{3,2,1,0:T(8,128)S(1)}, u32[]{:S(2)}, u32[]{:S(2)}) async-start(f32[16,2,128,128]{3,2,1,0:T(8,128)} %copy-done.1), calls=%async_computation.3 | async-start | bytes 4194304 | tf_op jit(solution)/shard_map/all_to_all | solution.py:614
  184.2 1.2 copy-start.4
  192.3 1.3 copy-start
  193.6 42.8 %copy-start.6 = (bf16[8,256,256]{2,1,0:T(8,128)(2,1)S(1)}, bf16[8,256,256]{2,1,0:T(8,128)(2,1)}, u32[]{:S(2)}) copy-start(bf16[8,256,256]{2,1,0:T(8,128)(2,1)} %constant.92.clone.high_ref) | copy-start | bytes 3145732
  231.6 52.3 %all-to-all-start.4 = ((f32[16,2,128,128]{3,2,1,0:T(8,128)}), f32[16,2,128,128]{3,2,1,0:T(8,128)}, u32[]{:S(2)}, u32[]{:S(2)}) async-start(f32[16,2,128,128]{3,2,1,0:T(8,128)} %copy-done), calls=%async_computation.4 | async-start | bytes 4194304 | tf_op jit(solution)/shard_map/all_to_all | solution.py:624
  236.4 1.2 copy-start.7
  283.9 1.2 copy-start.8

commit v3 on v1

--- a/solution.py
+++ b/solution.py
@@ -313,54 +313,58 @@
     return dot(left[0], right[0]) + (dot(left[0], right[1]) + dot(left[1], right[0]))
 
 
-def deposit_kernel(slot_ref, cell_ref, mass_ref, *out_refs):
-    planes, tiles, per_tile = cell_ref.shape
+def pack_kernel(slot_ref, list_ref, *out_refs):
+    planes, tiles, size, _ = list_ref.shape
     groups, rows, _ = out_refs[0].shape
-    cap = rows // TR
-    row_id = lax.broadcasted_iota(jnp.int32, (TR, per_tile), 0)
-    col_id = lax.broadcasted_iota(jnp.int32, (TC, per_tile), 0)
+    cap = rows // size - 1
     for p in range(planes):
         out_ref = out_refs[p]
         out_ref[...] = jnp.zeros_like(out_ref)
-        total = jnp.sum(jnp.sum(mass_ref[p].astype(jnp.float32), axis=0, keepdims=True), axis=1, keepdims=True)
-        out_ref[:, cap * TR :, :] = jnp.broadcast_to(total[None], (groups, rows - cap * TR, TC))
-
-        def batch(g, _):
-            base = pl.multiple_of(g * 16, 16)
-            cells = cell_ref[p, pl.ds(base, 16), :]
-            weights = mass_ref[p, pl.ds(base, 16), :].astype(jnp.float32)
-            for i in range(16):
-                cell = cells[i : i + 1]
-                weight = weights[i : i + 1]
-                row_hot = jnp.where(row_id == cell // TC, weight, 0.0).astype(jnp.bfloat16)
-                col_hot = jnp.where(col_id == cell % TC, 1.0, 0.0).astype(jnp.bfloat16)
-                tile = lax.dot_general(
-                    row_hot, col_hot, (((1,), (1,)), ((), ())), preferred_element_type=jnp.float32
-                )
-                slot = slot_ref[p, base + i]
-                out_ref[slot // cap, pl.ds(pl.multiple_of((slot % cap) * TR, TR), TR), :] = tile
+        total = jnp.sum(list_ref[p, :, size // 2 :, :], axis=(0, 1))
+        total = jnp.sum(total.reshape(1, TC), axis=1, keepdims=True)
+        out_ref[:, cap * size :, :] = jnp.broadcast_to(total[None], (groups, size, TC))
+
+        def tile(t, _):
+            slot = slot_ref[p, t]
+            rows_at = pl.ds(pl.multiple_of((slot % cap) * size, size), size)
+            out_ref[slot // cap, rows_at, :] = list_ref[p, t]
             return 0
 
-        lax.fori_loop(0, tiles // 16, batch, 0)
-
-
-def assemble_kernel(place_ref, in_ref, out_ref, held):
+        lax.fori_loop(0, tiles, tile, 0)
+
+
+def assemble_kernel(size, place_ref, in_ref, out_ref, held):
     groups, rows, _ = in_ref.shape
-    cap = rows // TR
+    cap = rows // size - 1
     tiles = out_ref.shape[0]
+    half = size // 2
     held[...] = jnp.zeros_like(held)
-    total = in_ref[0, cap * TR : cap * TR + 1, 0:1]
+    total = in_ref[0, cap * size : cap * size + 1, 0:1]
     for s in range(1, groups):
-        total = total + in_ref[s, cap * TR : cap * TR + 1, 0:1]
+        total = total + in_ref[s, cap * size : cap * size + 1, 0:1]
+    row_id = lax.broadcasted_iota(jnp.int32, (TR, TC), 0)
+    col_id = lax.broadcasted_iota(jnp.int32, (TC, TC), 0)
 
     def source(s, _):
         for c in range(cap):
             at = place_ref[s * cap + c]
-            held[at] = held[at] + in_ref[s, c * TR : (c + 1) * TR, :]
+            entry = in_ref[s, c * size : (c + 1) * size, :]
+            cells = entry[:half].astype(jnp.int32)
+            row_hot, col_hot = [], []
+            for i in range(half):
+                cell = cells[i : i + 1]
+                row_hot.append(jnp.where(row_id == cell // TC, entry[half + i : half + i + 1], 0.0))
+                col_hot.append(jnp.where(col_id == cell % TC, 1.0, 0.0))
+            held[at] = held[at] + lax.dot_general(
+                jnp.concatenate(row_hot, axis=1).astype(jnp.bfloat16),
+                jnp.concatenate(col_hot, axis=1).astype(jnp.bfloat16),
+                (((1,), (1,)), ((), ())),
+                preferred_element_type=jnp.float32,
+            )
         return 0
 
     lax.fori_loop(0, groups, source, 0)
-    factor = (L * L) / total
+    factor = jnp.where(total > 0.0, (L * L) / total, 0.0)
     out_ref[...] = held[0:tiles] * factor[None] - 1.0
 
 
@@ -532,35 +536,44 @@
     other_coef = jnp.where(mine_shell > 0, other[:planes], 0.0)
     other_dist = other[planes:]
 
-    table = block_tile.reshape(planes, groups, local_tiles)
-    owner = table // per_owner
     earlier = jnp.arange(local_tiles)[:, None] < jnp.arange(local_tiles)[None, :]
-    same_owner = owner[:, :, :, None] == owner[:, :, None, :]
-    rank = jnp.sum(jnp.where(same_owner & earlier[None, None], 1, 0), axis=2)
-    slot = owner * cap + rank
+    wanted = me * cap + jnp.arange(cap)
+
+    def routes(tiles):
+        table = tiles.reshape(planes, groups, local_tiles)
+        owner = table // per_owner
+        same_owner = owner[:, :, :, None] == owner[:, :, None, :]
+        rank = jnp.sum(jnp.where(same_owner & earlier[None, None], 1, 0), axis=2)
+        slot = owner * cap + rank
+        here = slot[:, :, None, :] == wanted[None, None, :, None]
+        local_index = table - me * per_owner
+        place = jnp.sum(jnp.where(here, local_index[:, :, None, :] + 1, 0), axis=3)
+        place = jnp.where(place > 0, place - 1, per_owner).reshape(planes, groups * cap)
+        return slot, place
+
+    slot, place = routes(block_tile)
+    _, other_place = routes(lax.ppermute(block_tile, "shell", pairs))
     my_slots = lax.dynamic_index_in_dim(slot, me, axis=1, keepdims=False)
-    wanted = me * cap + jnp.arange(cap)
-    here = slot[:, :, None, :] == wanted[None, None, :, None]
-    local_index = table - me * per_owner
-    place = jnp.sum(jnp.where(here, local_index[:, :, None, :] + 1, 0), axis=3)
-    place = jnp.where(place > 0, place - 1, per_owner).reshape(planes, groups * cap)
-
-    rows = cap * TR + 8
-    outgoing = call(deposit_kernel, [shape(groups, rows, TC)] * planes, count=3, flops=1 << 29)(
-        my_slots, cell_index, masses
-    )
+
+    half = per_tile // TC
+    as_lists = lambda part: part.astype(jnp.float32).reshape(planes, local_tiles, half, TC)
+    lists = jnp.concatenate([as_lists(cell_index), as_lists(masses)], axis=2)
+    outgoing = call(
+        pack_kernel, [shape(groups, (cap + 1) * 2 * half, TC)] * planes, count=2, flops=1 << 20
+    )(my_slots, lists)
+    deposit = lambda where, entries: call(
+        partial(assemble_kernel, 2 * half),
+        shape(per_owner, TR, TC),
+        [pltpu.VMEM((per_owner + 1, TR, TC), jnp.float32)],
+        count=2,
+        flops=1 << 31,
+    )(where, entries)
     near, far = [], []
     for p in range(planes):
         incoming = lax.all_to_all(outgoing[p], "pix", split_axis=0, concat_axis=0, tiled=True)
-        contrast = call(
-            assemble_kernel,
-            shape(per_owner, TR, TC),
-            [pltpu.VMEM((per_owner + 1, TR, TC), jnp.float32)],
-            count=2,
-            flops=1 << 22,
-        )(place[p], incoming)
-        near.append(contrast)
-        far.append(lax.ppermute(contrast, "shell", pairs))
+        passed = lax.ppermute(incoming, "shell", pairs)
+        near.append(deposit(place[p], incoming))
+        far.append(deposit(other_place[p], passed))
 
     own = plane_coef[None, :] * (1.0 - source_inv[:, None] * plane_dist[None, :])
     own = jnp.where(jnp.arange(planes)[None, :] <= jnp.arange(planes)[:, None], own, 0.0)
@@ -624,7 +637,7 @@
             shells == 2
             and cell_index.shape[0] == 2
             and groups == OUTER
-            and cell_index.shape[1] % 16 == 0
+            and cell_index.shape[2] % (4 * TC) == 0
         )
         return (local_fast if fits else local)(block_tile, cell_index, *rest)
 

time: 288 us -> 268 us (0.931)
  blocking collectives: 139 us -> 104 us
  Pallas kernels: 40 us -> 62.6 us
  waiting for transfers between devices: 80.1 us -> 64.3 us
  starting transfers between devices: 19.8 us -> 27.7 us
    all_to_all x1 -> x0, blocking collectives: 35.3 us -> none  [local_fast(): lax.all_to_all(outgoing[p], 'pix', split_axis=0, concat_axis=0, tiled=True)]
    pallas_call x3 -> x5, Pallas kernels: 9.58 us -> 32.3 us  [the longest x4 28.8 us: local_fast(): call(partial(assemble_kernel, 2 * half), shape(per_owner, TR, TC), [pltpu...]
    ppermute x1, waiting for transfers between devices: 21.4 us -> 0.68 us  [local_fast(): lax.ppermute(jnp.concatenate([plane_coef, plane_dist]), 'shell', pairs)]
    all_to_all x1 -> x2, starting transfers between devices: 3.88 us -> 11.5 us  [local_fast(): lax.all_to_all(outgoing[p], 'pix', split_axis=0, concat_axis=0, tiled=True)]
    all_to_all x1 -> x2, waiting for transfers between devices: 18 us -> 22.9 us  [local_fast(): lax.all_to_all(outgoing[p], 'pix', split_axis=0, concat_axis=0, tiled=True)]
    unnamed x28 -> x20, local copies, waits for them, and re-layouts: 3.13 us -> 0.05 us
    ppermute x2 -> x3, starting transfers between devices: 7.38 us -> 8.8 us  [the longest x2 4.87 us: local_fast(): passed = lax.ppermute(incoming, 'shell', pairs)]
  transfers between devices with their start and end apart: 5 -> 7, of which waited for: 3 -> 4; matrix products, arithmetic and copies ran while one was open for 1% -> 2% of each run, Pallas kernels for 1% -> 8%
where the time goes in v3:
time: 268 us; the launch traced here: 267 us
  blocking collectives  104 us (39%)
  waiting for transfers between devices  64.3 us (24%)
  Pallas kernels  62.6 us (23%)
  starting transfers between devices  27.7 us (10%)
  other arithmetic  4.26 us (2%)
  local copies, waits for them, and re-layouts  3.75 us (1%)
    all_to_all x1, blocking collectives, local_fast(): lax.all_to_all(leaving, 'pix', split_axis=0, concat_axis=0, tiled=True)  104 us
    all_to_all x1, waiting for transfers between devices, local_fast(): lax.all_to_all(sending.reshape(groups, 2, slab, INNER), 'pix', split_axis...  40.7 us
    pallas_call x4, Pallas kernels, local_fast(): call(partial(assemble_kernel, 2 * half), shape(per_owner, TR, TC), [pltpu...  28.8 us
    all_to_all x2, waiting for transfers between devices, local_fast(): lax.all_to_all(outgoing[p], 'pix', split_axis=0, concat_axis=0, tiled=True)  22.9 us
    pallas_call x1, Pallas kernels, local_fast(): call(column_kernel, shape(groups, 2, 2, slab, INNER), [pltpu.VMEM((OUTER,...  13.8 us
    all_to_all x2, starting transfers between devices, local_fast(): lax.all_to_all(outgoing[p], 'pix', split_axis=0, concat_axis=0, tiled=True)  11.5 us
    pallas_call x1, Pallas kernels, local_fast(): call(row_inverse_kernel, [shape(planes, slab, L)] * 2, [pltpu.VMEM((HALF_...  10.2 us
    pallas_call x1, Pallas kernels, local_fast(): call(row_forward_kernel, [shape(planes, slab, L), shape(HALF_BLOCKS, plan...  6.23 us
  transfers between devices with their start and end apart: 7, of which 4 were waited for; matrix products, arithmetic and copies ran while one was open for 2% of the time, Pallas kernels for 8%

profile of v3, /device:TPU:1, one launch (start us, length us, event | category | flops | bytes accessed | tf_op | source)
XLA Modules:
  0.0 267.1 jit_solution(12473461303227991477)
XLA Ops:
  0.6 3.9 %collective-permute-start.1 = (s32[2,1024]{1,0:T(2,128)}, s32[2,1024]{1,0:T(2,128)S(1)}, u32[]{:S(2)}, u32[]{:S(2)}) collective-permute-start(s32[2,1024]{1,0:T(2,128)} %param.15), channel_id=1, source_target_pairs={{0,16},{1,17},{2,18},{3,19},{4,20},{5,21},{6,22},{7,23},{8,24},{9,... | collective-permute-start | bytes 24584 | tf_op jit(solution)/shard_map/ppermute | solution.py:555
  4.6 0.8 reshape.212
  5.4 1.0 convert_element_type.4
  6.4 0.1 reshape.213
  6.5 1.0 reshape.220
  7.5 0.1 pad_maximum_fusion.list_ref
  7.7 0.8 select_reduce_fusion
  8.6 3.5 %shard_map.166 = (f32[16,72,128]{2,1,0:T(8,128)}, f32[16,72,128]{2,1,0:T(8,128)}) custom-call(s32[2,64]{1,0:T(2,128)S(1)} %bitcast.3, f32[2,64,8,128]{3,2,1,0:T(8,128)S(1)} %pad_maximum_fusion.list_ref), custom_call_target="tpu_custom_call" | custom-call | flops 1048576 | bytes 4194304 | tf_op jit(solution)/shard_map/pallas_call | solution.py:561
  12.1 6.8 %all-to-all-start.1 = ((f32[16,72,128]{2,1,0:T(8,128)}), f32[16,72,128]{2,1,0:T(8,128)S(1)}, u32[]{:S(2)}, u32[]{:S(2)}) async-start(f32[16,72,128]{2,1,0:T(8,128)} %get-tuple-element.10), calls=%async_computation.1 | async-start | bytes 1179648 | tf_op jit(solution)/shard_map/all_to_all | solution.py:573
  19.0 2.4 collective-permute-start
  21.4 0.7 collective-permute-done
  22.2 11.9 %all-to-all-done.1.in_ref = f32[16,72,128]{2,1,0:T(8,128)S(1)} async-done(((f32[16,72,128]{2,1,0:T(8,128)}), f32[16,72,128]{2,1,0:T(8,128)S(1)}, u32[]{:S(2)}, u32[]{:S(2)}) %all-to-all-start.1) | async-done | bytes 589856 | tf_op jit(solution)/shard_map/all_to_all | solution.py:573
  34.1 4.7 %all-to-all-start = ((f32[16,72,128]{2,1,0:T(8,128)}), f32[16,72,128]{2,1,0:T(8,128)S(1)}, u32[]{:S(2)}, u32[]{:S(2)}) async-start(f32[16,72,128]{2,1,0:T(8,128)} %get-tuple-element.9), calls=%async_computation | async-start | bytes 1179648 | tf_op jit(solution)/shard_map/all_to_all | solution.py:573
  38.8 1.2 select_reduce_fusion.2
  40.1 0.1 squeeze.21.place_ref
  40.2 2.4 collective-permute-start.3
  42.8 0.1 squeeze.18.place_ref
  42.9 11.0 %all-to-all-done.in_ref = f32[16,72,128]{2,1,0:T(8,128)S(1)} async-done(((f32[16,72,128]{2,1,0:T(8,128)}), f32[16,72,128]{2,1,0:T(8,128)S(1)}, u32[]{:S(2)}, u32[]{:S(2)}) %all-to-all-start) | async-done | bytes 589856 | tf_op jit(solution)/shard_map/all_to_all | solution.py:573
  53.9 2.4 collective-permute-start.2
  56.4 7.2 %shard_map.168.near1 = f32[128,16,128]{2,1,0:T(8,128)S(1)} custom-call(s32[128]{0:T(128)S(1)} %squeeze.20.place_ref, f32[16,72,128]{2,1,0:T(8,128)S(1)} %all-to-all-done.1.in_ref), custom_call_target="tpu_custom_call" | custom-call | flops 2147483648 | bytes 4194304 | tf_op jit(solution)/shard_map/pallas_call | solution.py:564
  63.5 7.2 %shard_map.167.near0 = f32[128,16,128]{2,1,0:T(8,128)S(1)} custom-call(s32[128]{0:T(128)S(1)} %squeeze.18.place_ref, f32[16,72,128]{2,1,0:T(8,128)S(1)} %all-to-all-done.in_ref), custom_call_target="tpu_custom_call" | custom-call | flops 2147483648 | bytes 4194304 | tf_op jit(solution)/shard_map/pallas_call | solution.py:564
  70.7 7.2 %shard_map.170.far1 = f32[128,16,128]{2,1,0:T(8,128)S(1)} custom-call(s32[128]{0:T(128)S(1)} %squeeze.22.place_ref, f32[16,72,128]{2,1,0:T(8,128)S(1)} %collective-permute-done.3.in_ref), custom_call_target="tpu_custom_call" | custom-call | flops 2147483648 | bytes 4194304 | tf_op jit(solution)/shard_map/pallas_call | solution.py:564
  78.0 7.2 %shard_map.169.far0 = f32[128,16,128]{2,1,0:T(8,128)S(1)} custom-call(s32[128]{0:T(128)S(1)} %squeeze.21.place_ref, f32[16,72,128]{2,1,0:T(8,128)S(1)} %collective-permute-done.2.in_ref), custom_call_target="tpu_custom_call" | custom-call | flops 2147483648 | bytes 4194304 | tf_op jit(solution)/shard_map/pallas_call | solution.py:564
  85.2 6.2 %shard_map.171 = (f32[2,128,2048]{2,1,0:T(8,128)}, f32[8,2,2,128,128]{4,3,2,1,0:T(8,128)}) custom-call(f32[2,4]{1,0:T(2,128)S(1)} %pad_maximum_fusion.1.mix_ref, f32[128,16,128]{2,1,0:T(8,128)S(1)} %shard_map.167.near0, f32[128,16,128]{2,1,0:T(8,128)S(1)} %shard_map.168.near1, f32[128,16,128]{2,1,0:T(8,128)S(1)} %shard_map.169.far0, ...), custom_call_target="tpu_custom_call" | custom-call | flops 1073741824 | bytes 4194304 | tf_op jit(solution)/shard_map/pallas_call | solution.py:584
  91.5 5.0 %all-to-all-start.2 = ((f32[16,2,128,128]{3,2,1,0:T(8,128)}), f32[16,2,128,128]{3,2,1,0:T(8,128)S(1)}, u32[]{:S(2)}, u32[]{:S(2)}) async-start(f32[16,2,128,128]{3,2,1,0:T(8,128)} %bitcast.5), calls=%async_computation.2 | async-start | bytes 4194304 | tf_op jit(solution)/shard_map/all_to_all | solution.py:591
  96.5 0.8 compare_select_fusion
  97.3 40.7 %all-to-all-done.2.in_ref = f32[16,2,128,128]{3,2,1,0:T(8,128)S(1)} async-done(((f32[16,2,128,128]{3,2,1,0:T(8,128)}), f32[16,2,128,128]{3,2,1,0:T(8,128)S(1)}, u32[]{:S(2)}, u32[]{:S(2)}) %all-to-all-start.2) | async-done | bytes 2097184 | tf_op jit(solution)/shard_map/all_to_all | solution.py:591
  138.0 1.1 broadcast_in_dim.93.twr_ref
  139.1 0.3 broadcast_in_dim.94.twi_ref
  139.5 13.8 %shard_map.172 = f32[16,2,2,128,128]{4,3,2,1,0:T(8,128)} custom-call(f32[16,2,128,128]{3,2,1,0:T(8,128)S(1)} %all-to-all-done.2.in_ref, f32[2,128]{1,0:T(2,128)S(1)} %pad_maximum_fusion.2.col_ref, f32[16,128,128]{2,1,0:T(8,128)S(1)} %broadcast_in_dim.93.twr_ref, f32[16,128,128]{2,1,0:T(8,128)S(1)} %broadcast_in_dim.94.twi_ref, ...), custom_call_target="tpu_custom_call" | custom-call | flops 2147483648 | bytes 4194304 | tf_op jit(solution)/shard_map/pallas_call | solution.py:604
  153.3 103.6 %all_to_all.20 = f32[16,2,2,128,128]{4,3,2,1,0:T(8,128)} all-to-all(f32[16,2,2,128,128]{4,3,2,1,0:T(8,128)} %shard_map.172), channel_id=1, replica_groups=mesh['shell'=2,'pix'=16] {'pix'}, dimensions={0} | all-to-all | bytes 8388608 | tf_op jit(solution)/shard_map/all_to_all | solution.py:612
  256.9 10.2 %shard_map.173 = (f32[2,128,2048]{2,1,0:T(8,128)}, f32[2,128,2048]{2,1,0:T(8,128)}) custom-call(f32[8,2,2,2,128,128]{5,4,3,2,1,0:T(8,128)} %bitcast.4, bf16[8,256,256]{2,1,0:T(8,128)(2,1)S(1)} %copy-done.1, bf16[8,256,256]{2,1,0:T(8,128)(2,1)S(1)} %copy-done), custom_call_target="tpu_custom_call" | custom-call | flops 2147483648 | bytes 4194304 | tf_op jit(solution)/shard_map/pallas_call | solution.py:613
  (41 shorter events, 0.7 us)
Async XLA Ops:
  0.6 7.0 %collective-permute-start.1 = (s32[2,1024]{1,0:T(2,128)}, s32[2,1024]{1,0:T(2,128)S(1)}, u32[]{:S(2)}, u32[]{:S(2)}) collective-permute-start(s32[2,1024]{1,0:T(2,128)} %param.15), channel_id=1, source_target_pairs={{0,16},{1,17},{2,18},{3,19},{4,20},{5,21},{6,22},{7,23},{8,24},{9,... | collective-permute-start | bytes 24584 | tf_op jit(solution)/shard_map/ppermute | solution.py:555
  6.4 12.5 %copy-start.7 = (f32[2]{0:T(128)S(1)}, f32[2]{0:T(128)}, u32[]{:S(2)}) copy-start(f32[2]{0:T(128)} %param.19) | copy-start | bytes 28
  6.4 12.5 %copy-start.8 = (f32[2]{0:T(128)S(1)}, f32[2]{0:T(128)}, u32[]{:S(2)}) copy-start(f32[2]{0:T(128)} %param.18) | copy-start | bytes 28
  6.4 15.8 %copy-start.9 = (f32[2]{0:T(128)S(1)}, f32[2]{0:T(128)}, u32[]{:S(2)}) copy-start(f32[2]{0:T(128)} %param.20) | copy-start | bytes 28
  12.1 22.0 %all-to-all-start.1 = ((f32[16,72,128]{2,1,0:T(8,128)}), f32[16,72,128]{2,1,0:T(8,128)S(1)}, u32[]{:S(2)}, u32[]{:S(2)}) async-start(f32[16,72,128]{2,1,0:T(8,128)} %get-tuple-element.10), calls=%async_computation.1 | async-start | bytes 1179648 | tf_op jit(solution)/shard_map/all_to_all | solution.py:573
  19.0 3.1 %collective-permute-start = (f32[4]{0:T(128)S(1)}, f32[4]{0:T(128)S(1)}, u32[]{:S(2)}, u32[]{:S(2)}) collective-permute-start(f32[4]{0:T(128)S(1)} %pad_maximum_fusion.3), channel_id=1, source_target_pairs={{0,16},{1,17},{2,18},{3,19},{4,20},{5,21},{6,22},{7,23},{8,24},{9,... | collective-permute-start | bytes 56 | tf_op jit(solution)/shard_map/ppermute | solution.py:535
  34.1 19.8 %all-to-all-start = ((f32[16,72,128]{2,1,0:T(8,128)}), f32[16,72,128]{2,1,0:T(8,128)S(1)}, u32[]{:S(2)}, u32[]{:S(2)}) async-start(f32[16,72,128]{2,1,0:T(8,128)} %get-tuple-element.9), calls=%async_computation | async-start | bytes 1179648 | tf_op jit(solution)/shard_map/all_to_all | solution.py:573
  40.2 30.5 %collective-permute-start.3 = (f32[16,72,128]{2,1,0:T(8,128)S(1)}, f32[16,72,128]{2,1,0:T(8,128)S(1)}, u32[]{:S(2)}, u32[]{:S(2)}) collective-permute-start(f32[16,72,128]{2,1,0:T(8,128)S(1)} %all-to-all-done.1.in_ref), channel_id=1, source_target_pairs={{0,16},{1,17},{2,18},{3,19},{4,20},{5,21},{6,22},{7,23},{8,24},{9,... | collective-permute-start | bytes 1769480 | tf_op jit(solution)/shard_map/ppermute | solution.py:574
  53.9 24.1 %collective-permute-start.2 = (f32[16,72,128]{2,1,0:T(8,128)S(1)}, f32[16,72,128]{2,1,0:T(8,128)S(1)}, u32[]{:S(2)}, u32[]{:S(2)}) collective-permute-start(f32[16,72,128]{2,1,0:T(8,128)S(1)} %all-to-all-done.in_ref), channel_id=1, source_target_pairs={{0,16},{1,17},{2,18},{3,19},{4,20},{5,21},{6,22},{7,23},{8,24},{9,... | collective-permute-start | bytes 1769480 | tf_op jit(solution)/shard_map/ppermute | solution.py:574
  78.0 7.3 %copy-start.1 = (bf16[8,256,256]{2,1,0:T(8,128)(2,1)S(1)}, bf16[8,256,256]{2,1,0:T(8,128)(2,1)}, u32[]{:S(2)}) copy-start(bf16[8,256,256]{2,1,0:T(8,128)(2,1)} %constant.100.clone.high_ref) | copy-start | bytes 3145732
  91.5 47.6 %copy-start.6 = (f32[16,128]{1,0:T(8,128)S(1)}, f32[16,128]{1,0:T(8,128)}, u32[]{:S(2)}) copy-start(f32[16,128]{1,0:T(8,128)} %constant.104.clone) | copy-start | bytes 24580
  91.5 46.6 %all-to-all-start.2 = ((f32[16,2,128,128]{3,2,1,0:T(8,128)}), f32[16,2,128,128]{3,2,1,0:T(8,128)S(1)}, u32[]{:S(2)}, u32[]{:S(2)}) async-start(f32[16,2,128,128]{3,2,1,0:T(8,128)} %bitcast.5), calls=%async_computation.2 | async-start | bytes 4194304 | tf_op jit(solution)/shard_map/all_to_all | solution.py:591
  96.5 42.9 %copy-start.2 = (bf16[256,256]{1,0:T(8,128)(2,1)S(1)}, bf16[256,256]{1,0:T(8,128)(2,1)}, u32[]{:S(2)}) copy-start(bf16[256,256]{1,0:T(8,128)(2,1)} %constant.108.clone.back_low_ref) | copy-start | bytes 393220
  96.5 42.9 %copy-start.3 = (bf16[256,256]{1,0:T(8,128)(2,1)S(1)}, bf16[256,256]{1,0:T(8,128)(2,1)}, u32[]{:S(2)}) copy-start(bf16[256,256]{1,0:T(8,128)(2,1)} %constant.107.clone.back_high_ref) | copy-start | bytes 393220
  96.5 42.9 %copy-start.4 = (bf16[256,256]{1,0:T(8,128)(2,1)S(1)}, bf16[256,256]{1,0:T(8,128)(2,1)}, u32[]{:S(2)}) copy-start(bf16[256,256]{1,0:T(8,128)(2,1)} %constant.106.clone.low_ref) | copy-start | bytes 393220
  138.0 1.4 copy-start.5
  153.3 103.6 %copy-start = (bf16[8,256,256]{2,1,0:T(8,128)(2,1)S(1)}, bf16[8,256,256]{2,1,0:T(8,128)(2,1)}, u32[]{:S(2)}) copy-start(bf16[8,256,256]{2,1,0:T(8,128)(2,1)} %constant.101.clone.low_ref) | copy-start | bytes 3145732
